TPU v7x, 32 devices: a whole 2x2x4 slice. The times are simulated.
32 devices in a mesh: rep: 8 (over z, x), shard: 4 (over y, core).
Axes of the slice: x: 2, y: 2, z: 4, core: 2. Of those that a mesh axis runs over, the one named last changes fastest.
Arguments:
- inputs: bfloat16 [2560, 4096], P('rep', 'shard'), may hold values from -6 to 6
- weight: float32 [4096, 4096], P('shard', 'rep'), may hold values from -0.09375 to 0.09375
- table: bfloat16 [256, 4096], replicated, may hold values from -6 to 6
- targets: int32 [2560], P(('rep', 'shard')), may hold values from 0 to 255
Outputs:
- combined: float32 [4096, 4096], P('shard', 'rep')
- new_weight: float32 [4096, 4096], P('shard', 'rep')
All inputs are finite; a program needn't handle non-finite values.
Results may differ from a plain program's by a relative error of at most 0.005.
Values may be sent and summed in bfloat16 or wider, within the bound.
No kernel may reach another device: no remote copies, remote signals or barrier semaphores. Data moves between devices by JAX's collectives and lax.ppermute only.
A program may use at most 128 MiB of HBM per device.

v0:
```python
import functools

import jax
import jax.numpy as jnp
from jax import lax
from jax.experimental import pallas as pl
from jax.experimental.pallas import tpu as pltpu
from jax.sharding import PartitionSpec as P


epsilon = 1e-06
step_size = 0.05


def mix_pair(cross, norm_low, norm_high):
    norm_low = jnp.maximum(norm_low, 0.0)
    norm_high = jnp.maximum(norm_high, 0.0)
    bound = jnp.sqrt(norm_low) * jnp.sqrt(norm_high)
    cross = jnp.minimum(jnp.maximum(cross, -bound), bound)
    return (
        1.0 - cross / (2.0 * (norm_low + epsilon)),
        1.0 - cross / (2.0 * (norm_high + epsilon)),
    )


def tree_weights(entry, count):
    products = {(a, b): entry(a, b) for a in range(count) for b in range(a, count)}
    weights = [None] * count
    group = 1
    alive = count
    while alive > 1:
        factors = []
        for m in range(alive // 2):
            low, high = mix_pair(
                products[2 * m, 2 * m + 1], products[2 * m, 2 * m], products[2 * m + 1, 2 * m + 1]
            )
            factors.append((low, high))
            for r in range(2 * m * group, (2 * m + 1) * group):
                weights[r] = low if weights[r] is None else weights[r] * low
            for r in range((2 * m + 1) * group, (2 * m + 2) * group):
                weights[r] = high if weights[r] is None else weights[r] * high
        merged = {}
        for a in range(alive // 2):
            for b in range(a, alive // 2):
                terms = [
                    factors[a][i]
                    * factors[b][j]
                    * products[min(2 * a + i, 2 * b + j), max(2 * a + i, 2 * b + j)]
                    for i in range(2)
                    for j in range(2)
                ]
                merged[a, b] = (terms[0] + terms[3]) + (terms[1] + terms[2])
        products = merged
        alive //= 2
        group *= 2
    return weights


def grad_kernel(where, *refs, news, olds):
    xs = refs[: 2 * news]
    own, other = refs[2 * news : 2 * news + 2]
    old = refs[2 * news + 2 : 2 * news + 2 + olds]
    new = refs[2 * news + 2 + olds : 2 * news + 2 + olds + news]
    sums = refs[-1]
    for n in range(news):
        new[n][...] = lax.dot_general(
            jnp.concatenate([xs[2 * n][...], xs[2 * n + 1][...]], axis=0),
            jnp.concatenate([own[n, 0], own[n, 1], other[n, 0], other[n, 1]], axis=0),
            (((0,), (0,)), ((), ())),
            preferred_element_type=jnp.float32,
        )
    every = list(old) + list(new)
    pairs = [(i, olds + n) for n in range(news) for i in range(olds + n + 1)]
    features, columns = new[0].shape

    def body(step, carry):
        carry = list(carry)
        for c in range(columns // 128):
            got = [ref[pl.ds(pl.multiple_of(step * 8, 8), 8), c * 128 : (c + 1) * 128] for ref in every]
            for k, (i, j) in enumerate(pairs):
                carry[k] = carry[k] + got[i] * got[j]
        return tuple(carry)

    totals = lax.fori_loop(
        0, features // 8, body, tuple(jnp.zeros((8, 128), jnp.float32) for _ in pairs), unroll=4
    )
    for k in range(len(pairs)):
        sums[k] = totals[k]


def ring_replica(index, count):
    return jnp.where(index < count // 2, 2 * index, 2 * (count - 1 - index) + 1)


def ring_place(replica, count):
    return jnp.where(replica % 2 == 0, replica // 2, count - 1 - replica // 2)


def replica_at(rep, offset, count):
    index = ring_place(rep, count) + offset % count
    return ring_replica(jnp.where(index >= count, index - count, index), count)


def place_kernel(where, *refs, pairs, offsets):
    out = refs[-1]
    count = len(offsets)
    ids = [replica_at(where[0], offset, count) for offset in offsets]
    row = lax.broadcasted_iota(jnp.int32, (8, 128), 0)
    column = lax.broadcasted_iota(jnp.int32, (8, 128), 1)
    tile = jnp.zeros((8, 128), jnp.float32)
    at = 0
    for ref in refs[:-1]:
        for k in range(ref.shape[0]):
            i, j = pairs[at]
            at += 1
            total = jnp.sum(ref[k], axis=(0, 1), keepdims=True)
            here = ((row == ids[i]) & (column == ids[j])) | ((row == ids[j]) & (column == ids[i]))
            tile = jnp.where(here, total, tile)
    out[...] = tile


def combine_kernel(where, products, weight, *refs, offsets, tile):
    count = len(offsets)
    grads = refs[:count]
    combined, new_weight, factors = refs[count:]

    @pl.when(pl.program_id(0) == 0)
    def _():
        weights = tree_weights(lambda a, b: jnp.full((8, 128), products[a, b], jnp.float32), count)
        for i, offset in enumerate(offsets):
            mine = replica_at(where[0], offset, count)
            value = weights[0]
            for a in range(1, count):
                value = jnp.where(mine == a, weights[a], value)
            factors[i] = value

    local = [factors[i] for i in range(count)]
    columns = combined.shape[1] // 128

    def body(step, carry):
        rows = pl.ds(pl.multiple_of(step * 8, 8), 8)
        for c in range(columns):
            lanes = slice(c * 128, (c + 1) * 128)
            total = local[0] * grads[0][rows, lanes]
            for i in range(1, count):
                total = total + local[i] * grads[i][rows, lanes]
            combined[rows, lanes] = total
            new_weight[rows, lanes] = weight[rows, lanes] - step_size * total
        return carry

    lax.fori_loop(0, tile // 8, body, 0, unroll=4)


def local_call(kernel, shapes, *args):
    vmem = pl.BlockSpec(memory_space=pltpu.VMEM)
    out = pl.pallas_call(
        kernel,
        in_specs=[pl.BlockSpec(memory_space=pltpu.SMEM)] + [vmem] * (len(args) - 1),
        out_specs=[vmem] * len(shapes),
        out_shape=[jax.ShapeDtypeStruct(shape, dtype) for shape, dtype in shapes],
        compiler_params=pltpu.CompilerParams(vmem_limit_bytes=12 * 2**20),
    )(*args)
    return out


def rows_kernel(where, inputs, mine, theirs):
    core = where[1] & 1
    quarter = mine.shape[0] // 2
    for y in range(2):
        for out, side in ((mine, core), (theirs, 1 - core)):
            start = pl.multiple_of((2 * y + side) * quarter, quarter)
            out[y * quarter : (y + 1) * quarter] = inputs[pl.ds(start, quarter)]


def cast_kernel(where, weight, weight_b):
    weight_b[...] = weight[...].astype(weight_b.dtype)


def outputs_kernel(where, *refs):
    news = (len(refs) - 4) // 2
    weight_b, weight_other, keep, send = refs[2 * news :]
    quarter = keep.shape[1]
    upper = where[1] >> 1 == 1
    for n in range(news):
        made = jnp.dot(refs[n][...], weight_b[...], preferred_element_type=jnp.float32)
        made += jnp.dot(refs[news + n][...], weight_other[...], preferred_element_type=jnp.float32)
        first, second = made[:quarter], made[quarter:]
        keep[n] = jnp.where(upper, second, first)
        send[n] = jnp.where(upper, first, second)


def error_kernel(where, mine, got, wanted, error, *, at, rows):
    for n in range(error.shape[0]):
        error[n] = ((mine[n] + got[n] - wanted[at + n]) / rows).astype(error.dtype)


def pair_kernel(where, mine, got, pair):
    upper = where[1] >> 1 == 1
    for n in range(pair.shape[0]):
        pair[n, 0] = jnp.where(upper, got[n], mine[n])
        pair[n, 1] = jnp.where(upper, mine[n], got[n])


def wanted_kernel(where, *refs, offsets):
    targets, table, wanted = refs
    count = len(offsets)
    candidates = lax.broadcasted_iota(jnp.int32, (table.shape[0], wanted.shape[1]), 0)
    for i, offset in enumerate(offsets):
        slot = replica_at(where[0], offset, count) ^ where[0]
        chosen = targets[0:1]
        for k in range(1, count):
            chosen = jnp.where(slot == k, targets[k : k + 1], chosen)
        hot = (candidates == chosen).astype(table.dtype)
        wanted[i] = lax.dot_general(
            hot, table[...], (((0,), (0,)), ((), ())), preferred_element_type=jnp.float32
        )


def ring_path(inputs, weight, table, targets):
    count = lax.axis_size("rep")
    rows = inputs.shape[0]
    features, columns = weight.shape
    quarter = rows // 4
    right = []
    left = []
    for i in range(count):
        ends = [2 * r if r < count // 2 else 2 * (count - 1 - r) + 1 for r in (i, (i + 1) % count)]
        right.append((ends[0], ends[1]))
        left.append((ends[1], ends[0]))
    far = count // 2
    where = jnp.stack([lax.axis_index("rep"), lax.axis_index("shard")])

    half = ((rows // 2, features), inputs.dtype)
    from_left = [local_call(rows_kernel, (half, half), where, inputs)]
    from_right = [from_left[0]]
    for step in range(1, far + 1):
        last = step == far
        a = lax.ppermute(from_left[-1][0], "rep", right)
        d = lax.ppermute(from_right[-1][1], "rep", left)
        b = None if last else lax.ppermute(from_left[-1][1], "rep", right)
        c = None if last else lax.ppermute(from_right[-1][0], "rep", left)
        from_left.append([a, b])
        from_right.append([c, d])
    phases = [[(0, from_left[0])]]
    for step in range(1, far):
        phases.append([(-step, from_left[step]), (step, from_right[step])])
    phases.append([(far, [from_left[far][0], from_right[far][1]])])
    offsets = tuple(offset for phase in phases for offset, _ in phase)

    all_targets = targets[None]
    for i in range(count.bit_length() - 1):
        pairs = [(r, r ^ 1 << i) for r in range(count)]
        all_targets = jnp.concatenate([all_targets, lax.ppermute(all_targets, "rep", pairs)])
    wanted = pl.pallas_call(
        functools.partial(wanted_kernel, offsets=offsets),
        grid_spec=pltpu.PrefetchScalarGridSpec(
            num_scalar_prefetch=1,
            grid=(1,),
            in_specs=[
                pl.BlockSpec((count, quarter), lambda i, where: (0, 0)),
                pl.BlockSpec((table.shape[0], columns), lambda i, where: (0, where[0])),
            ],
            out_specs=pl.BlockSpec((count, quarter, columns), lambda i, where: (0, 0, 0)),
        ),
        out_shape=jax.ShapeDtypeStruct((count, quarter, columns), jnp.float32),
        compiler_params=pltpu.CompilerParams(vmem_limit_bytes=8 * 2**20),
        name="wanted",
    )(where, all_targets, table)

    swap_core = [(i, i ^ 1) for i in range(4)]
    swap_y = [(i, i ^ 2) for i in range(4)]
    grads = []
    sums = []
    pairs = []
    at = 0
    (weight_b,) = local_call(cast_kernel, ((weight.shape, jnp.bfloat16),), where, weight)
    weight_other = lax.ppermute(weight_b, "shard", swap_core)
    for phase in phases:
        xs = [x for _, chunk in phase for x in chunk]
        news = len(phase)
        whole = ((news, 2, quarter, columns), jnp.bfloat16)
        part = ((news, quarter, columns), jnp.float32)
        others = [lax.ppermute(x, "shard", swap_core) for x in xs[1::2]]
        keep, send = local_call(
            outputs_kernel, (part, part), where, *xs[::2], *others, weight_b, weight_other
        )
        got = lax.ppermute(send, "shard", swap_y)
        (error,) = local_call(
            functools.partial(error_kernel, at=at, rows=rows),
            ((part[0], jnp.bfloat16),),
            where,
            keep,
            got,
            wanted,
        )
        got = lax.ppermute(error, "shard", swap_y)
        (own,) = local_call(pair_kernel, (whole,), where, error, got)
        other = lax.ppermute(own, "shard", swap_core)
        fresh = [(i, at + n) for n in range(news) for i in range(at + n + 1)]
        made = local_call(
            functools.partial(grad_kernel, news=news, olds=at),
            ((weight.shape, jnp.float32),) * news + (((len(fresh), 8, 128), jnp.float32),),
            where,
            *xs,
            own,
            other,
            *grads,
        )
        pairs += fresh
        grads = grads + list(made[:news])
        sums.append(made[news])
        at += news

    (products,) = local_call(
        functools.partial(place_kernel, pairs=pairs, offsets=offsets),
        (((8, 128), jnp.float32),),
        where,
        *sums,
    )
    products = products + lax.ppermute(products, "shard", swap_core)
    products = products + lax.ppermute(products, "shard", swap_y)
    bit = 1
    while bit < count:
        products = products + lax.ppermute(products, "rep", [(i, i ^ bit) for i in range(count)])
        bit *= 2
    tile = features // 4
    smem = pl.BlockSpec(memory_space=pltpu.SMEM)
    block = pl.BlockSpec((tile, columns), lambda i: (i, 0))
    return pl.pallas_call(
        functools.partial(combine_kernel, offsets=offsets, tile=tile),
        grid=(features // tile,),
        in_specs=[smem, smem] + [block] * (1 + count),
        out_specs=[block, block],
        out_shape=[jax.ShapeDtypeStruct((features, columns), jnp.float32)] * 2,
        scratch_shapes=[pltpu.VMEM((count, 8, 128), jnp.float32)],
        compiler_params=pltpu.CompilerParams(
            dimension_semantics=("arbitrary",), vmem_limit_bytes=16 * 2**20
        ),
        name="combine",
    )(where, products, weight, *grads)


def gather_path(inputs, weight, table, targets):
    count = lax.axis_size("rep")
    rows = inputs.shape[0]
    features, columns = weight.shape
    rep = lax.axis_index("rep")
    all_inputs = lax.all_gather(inputs, "rep", axis=0, tiled=True)
    all_targets = lax.all_gather(targets, "rep", axis=0, tiled=False)
    partial = jnp.dot(all_inputs, weight.astype(jnp.bfloat16), preferred_element_type=jnp.float32)
    outputs = lax.psum_scatter(
        partial.reshape(count, rows, columns), "shard", scatter_dimension=1, tiled=True
    )
    table_columns = lax.dynamic_slice(table, (0, rep * columns), (table.shape[0], columns))
    wanted = table_columns[all_targets].astype(jnp.float32)
    error = ((outputs - wanted) / rows).astype(jnp.bfloat16)
    errors = lax.all_gather(error, "shard", axis=1, tiled=True)
    grads = lax.dot_general(
        all_inputs.reshape(count, rows, features),
        errors,
        (((1,), (1,)), ((0,), (0,))),
        preferred_element_type=jnp.float32,
    )
    products = lax.dot_general(
        grads, grads, (((1, 2), (1, 2)), ((), ())), precision=lax.Precision.HIGHEST
    )
    products = lax.psum(products, ("rep", "shard"))
    weights = jnp.stack(tree_weights(lambda a, b: products[a, b], count))
    combined = jnp.sum(weights[:, None, None] * grads, axis=0)
    return combined, weight - step_size * combined


def solution(mesh):
    count, shards = mesh.shape["rep"], mesh.shape["shard"]
    ring = shards == 4 and count in (4, 8)

    def on_device(inputs, weight, table, targets):
        if ring:
            return tuple(ring_path(inputs, weight, table, targets))
        return gather_path(inputs, weight, table, targets)

    in_specs = (P("rep", "shard"), P("shard", "rep"), P(), P(("rep", "shard")))
    out_specs = (P("shard", "rep"), P("shard", "rep"))
    return jax.shard_map(
        on_device, mesh=mesh, in_specs=in_specs, out_specs=out_specs, check_vma=False
    )
```

profile of v0, /device:TPU:0, one launch (start us, length us, event | category | flops | bytes accessed | tf_op | source)
XLA Modules:
  0.0 142.8 jit_solution(7495302425553315949)
XLA Ops:
  2.4 3.0 %collective-permute-start.10 = (bf16[160,1024]{1,0:T(8,128)(2,1)S(1)}, bf16[160,1024]{1,0:T(8,128)(2,1)S(1)}, u32[]{:S(2)}, u32[]{:S(2)}) collective-permute-start(bf16[160,1024]{1,0:T(8,128)(2,1)S(1)} %get-tuple-element.27.refs_0_), channel_id=1, source_target_pairs={{8,0},{16,8},{24,16},{28,24},{20,28},{12,20},{4,12},{0,4},{9,1},{1... | collective-permute-start | bytes 983048 | tf_op jit(solution)/shard_map/ppermute | solution.py:241
  5.6 1.9 %collective-permute-start.11 = (bf16[160,1024]{1,0:T(8,128)(2,1)S(1)}, bf16[160,1024]{1,0:T(8,128)(2,1)S(1)}, u32[]{:S(2)}, u32[]{:S(2)}) collective-permute-start(bf16[160,1024]{1,0:T(8,128)(2,1)S(1)} %get-tuple-element.28.refs_1_), channel_id=1, source_target_pairs={{8,0},{16,8},{24,16},{28,24},{20,28},{12,20},{4,12},{0,4},{9,1},{1... | collective-permute-start | bytes 983048 | tf_op jit(solution)/shard_map/ppermute | solution.py:239
  10.6 3.5 %collective-permute-done.10.refs_1_.refs_2_ = bf16[160,1024]{1,0:T(8,128)(2,1)S(1)} collective-permute-done((bf16[160,1024]{1,0:T(8,128)(2,1)S(1)}, bf16[160,1024]{1,0:T(8,128)(2,1)S(1)}, u32[]{:S(2)}, u32[]{:S(2)}) %collective-permute-start.10) | collective-permute-done | bytes 327712 | tf_op jit(solution)/shard_map/ppermute | solution.py:241
  14.1 1.9 %collective-permute-start.19 = (bf16[160,1024]{1,0:T(8,128)(2,1)S(1)}, bf16[160,1024]{1,0:T(8,128)(2,1)S(1)}, u32[]{:S(2)}, u32[]{:S(2)}) collective-permute-start(bf16[160,1024]{1,0:T(8,128)(2,1)S(1)} %collective-permute-done.10.refs_1_.refs_2_), channel_id=1, source_target_pairs={{8,0},{16,8},{24,16},{28,24},{20,28},{12,20},{4,12},{0,4},{9,1},{1... | collective-permute-start | bytes 983048 | tf_op jit(solution)/shard_map/ppermute | solution.py:241
  16.1 4.4 %collective-permute-done.3 = s32[1,80]{1,0:T(1,128)S(1)} collective-permute-done((s32[1,80]{1,0:T(1,128)}, s32[1,80]{1,0:T(1,128)S(1)}, u32[]{:S(2)}, u32[]{:S(2)}) %collective-permute-start.3) | collective-permute-done | bytes 352 | tf_op jit(solution)/shard_map/ppermute | solution.py:253
  23.5 3.8 %collective-permute-done.4 = s32[2,80]{1,0:T(2,128)S(1)} collective-permute-done((s32[2,80]{1,0:T(2,128)S(1)}, s32[2,80]{1,0:T(2,128)S(1)}, u32[]{:S(2)}, u32[]{:S(2)}) %collective-permute-start.4) | collective-permute-done | bytes 672 | tf_op jit(solution)/shard_map/ppermute | solution.py:253
  27.3 3.0 %collective-permute-start.20 = (bf16[160,1024]{1,0:T(8,128)(2,1)S(1)}, bf16[160,1024]{1,0:T(8,128)(2,1)S(1)}, u32[]{:S(2)}, u32[]{:S(2)}) collective-permute-start(bf16[160,1024]{1,0:T(8,128)(2,1)S(1)} %collective-permute-done.11.refs_3_), channel_id=1, source_target_pairs={{8,0},{16,8},{24,16},{28,24},{20,28},{12,20},{4,12},{0,4},{9,1},{1... | collective-permute-start | bytes 983048 | tf_op jit(solution)/shard_map/ppermute | solution.py:239
  30.9 7.0 %collective-permute-done.20.refs_3_ = bf16[160,1024]{1,0:T(8,128)(2,1)S(1)} collective-permute-done((bf16[160,1024]{1,0:T(8,128)(2,1)S(1)}, bf16[160,1024]{1,0:T(8,128)(2,1)S(1)}, u32[]{:S(2)}, u32[]{:S(2)}) %collective-permute-start.20) | collective-permute-done | bytes 327712 | tf_op jit(solution)/shard_map/ppermute | solution.py:239
  37.9 2.5 %collective-permute-start.28 = (bf16[160,1024]{1,0:T(8,128)(2,1)S(1)}, bf16[160,1024]{1,0:T(8,128)(2,1)S(1)}, u32[]{:S(2)}, u32[]{:S(2)}) collective-permute-start(bf16[160,1024]{1,0:T(8,128)(2,1)S(1)} %collective-permute-done.19.refs_1_.refs_2_), channel_id=1, source_target_pairs={{8,0},{16,8},{24,16},{28,24},{20,28},{12,20},{4,12},{0,4},{9,1},{1... | collective-permute-start | bytes 983048 | tf_op jit(solution)/shard_map/ppermute | solution.py:241
  40.4 2.0 %collective-permute-start.29 = (bf16[160,1024]{1,0:T(8,128)(2,1)S(1)}, bf16[160,1024]{1,0:T(8,128)(2,1)S(1)}, u32[]{:S(2)}, u32[]{:S(2)}) collective-permute-start(bf16[160,1024]{1,0:T(8,128)(2,1)S(1)} %collective-permute-done.20.refs_3_), channel_id=1, source_target_pairs={{8,0},{16,8},{24,16},{28,24},{20,28},{12,20},{4,12},{0,4},{9,1},{1... | collective-permute-start | bytes 983048 | tf_op jit(solution)/shard_map/ppermute | solution.py:239
  42.5 6.0 %collective-permute-done.28.refs_1_.refs_2_ = bf16[160,1024]{1,0:T(8,128)(2,1)S(1)} collective-permute-done((bf16[160,1024]{1,0:T(8,128)(2,1)S(1)}, bf16[160,1024]{1,0:T(8,128)(2,1)S(1)}, u32[]{:S(2)}, u32[]{:S(2)}) %collective-permute-start.28) | collective-permute-done | bytes 327712 | tf_op jit(solution)/shard_map/ppermute | solution.py:241
  48.5 2.5 %collective-permute-done.26.refs_0_ = bf16[160,1024]{1,0:T(8,128)(2,1)S(1)} collective-permute-done((bf16[160,1024]{1,0:T(8,128)(2,1)S(1)}, bf16[160,1024]{1,0:T(8,128)(2,1)S(1)}, u32[]{:S(2)}, u32[]{:S(2)}) %collective-permute-start.26) | collective-permute-done | bytes 327712 | tf_op jit(solution)/shard_map/ppermute | solution.py:238
  51.0 3.2 %collective-permute-done.29.refs_3_ = bf16[160,1024]{1,0:T(8,128)(2,1)S(1)} collective-permute-done((bf16[160,1024]{1,0:T(8,128)(2,1)S(1)}, bf16[160,1024]{1,0:T(8,128)(2,1)S(1)}, u32[]{:S(2)}, u32[]{:S(2)}) %collective-permute-start.29) | collective-permute-done | bytes 327712 | tf_op jit(solution)/shard_map/ppermute | solution.py:239
  54.2 2.2 %collective-permute-done.27.refs_1_ = bf16[160,1024]{1,0:T(8,128)(2,1)S(1)} collective-permute-done((bf16[160,1024]{1,0:T(8,128)(2,1)S(1)}, bf16[160,1024]{1,0:T(8,128)(2,1)S(1)}, u32[]{:S(2)}, u32[]{:S(2)}) %collective-permute-start.27) | collective-permute-done | bytes 327712 | tf_op jit(solution)/shard_map/ppermute | solution.py:240
  67.2 2.7 %collective-permute-done.14.got = f32[2,80,512]{2,1,0:T(8,128)S(1)} collective-permute-done((f32[2,80,512]{2,1,0:T(8,128)S(1)}, f32[2,80,512]{2,1,0:T(8,128)S(1)}, u32[]{:S(2)}, u32[]{:S(2)}) %collective-permute-start.14) | collective-permute-done | bytes 327712 | tf_op jit(solution)/shard_map/ppermute | solution.py:287
  71.6 5.3 %collective-permute-done.23.got = f32[2,80,512]{2,1,0:T(8,128)S(1)} collective-permute-done((f32[2,80,512]{2,1,0:T(8,128)S(1)}, f32[2,80,512]{2,1,0:T(8,128)S(1)}, u32[]{:S(2)}, u32[]{:S(2)}) %collective-permute-start.23) | collective-permute-done | bytes 327712 | tf_op jit(solution)/shard_map/ppermute | solution.py:287
  79.0 4.9 %collective-permute-done.32.got = f32[2,80,512]{2,1,0:T(8,128)S(1)} collective-permute-done((f32[2,80,512]{2,1,0:T(8,128)S(1)}, f32[2,80,512]{2,1,0:T(8,128)S(1)}, u32[]{:S(2)}, u32[]{:S(2)}) %collective-permute-start.32) | collective-permute-done | bytes 327712 | tf_op jit(solution)/shard_map/ppermute | solution.py:287
  92.8 1.8 %collective-permute-done.33.got = bf16[2,80,512]{2,1,0:T(8,128)(2,1)S(1)} collective-permute-done((bf16[2,80,512]{2,1,0:T(8,128)(2,1)S(1)}, bf16[2,80,512]{2,1,0:T(8,128)(2,1)S(1)}, u32[]{:S(2)}, u32[]{:S(2)}) %collective-permute-start.33) | collective-permute-done | bytes 163872 | tf_op jit(solution)/shard_map/ppermute | solution.py:296
  95.2 2.9 %collective-permute-done.2.got = f32[1,80,512]{2,1,0:T(8,128)S(1)} collective-permute-done((f32[1,80,512]{2,1,0:T(8,128)S(1)}, f32[1,80,512]{2,1,0:T(8,128)S(1)}, u32[]{:S(2)}, u32[]{:S(2)}) %collective-permute-start.2) | collective-permute-done | bytes 163872 | tf_op jit(solution)/shard_map/ppermute | solution.py:287
  98.6 1.6 %collective-permute-start.6 = (bf16[1,80,512]{2,1,0:T(8,128)(2,1)S(1)}, bf16[1,80,512]{2,1,0:T(8,128)(2,1)S(1)}, u32[]{:S(2)}, u32[]{:S(2)}) collective-permute-start(bf16[1,80,512]{2,1,0:T(8,128)(2,1)S(1)} %shard_map.62.mine), channel_id=1, source_target_pairs={{0,2},{1,3},{2,0},{3,1},{4,6},{5,7},{6,4},{7,5},{8,10},{9,11},{10,... | collective-permute-start | bytes 245768 | tf_op jit(solution)/shard_map/ppermute | solution.py:296
  104.3 2.3 %collective-permute-done.39.got = bf16[1,80,512]{2,1,0:T(8,128)(2,1)S(1)} collective-permute-done((bf16[1,80,512]{2,1,0:T(8,128)(2,1)S(1)}, bf16[1,80,512]{2,1,0:T(8,128)(2,1)S(1)}, u32[]{:S(2)}, u32[]{:S(2)}) %collective-permute-start.39) | collective-permute-done | bytes 81952 | tf_op jit(solution)/shard_map/ppermute | solution.py:296
  107.3 1.9 %shard_map.64 = (f32[1024,512]{1,0:T(8,128)S(1)}, f32[1,8,128]{2,1,0:T(8,128)S(1)}) custom-call(s32[2]{0:T(128)S(1)} %pad_add_fusion.3.where, bf16[160,1024]{1,0:T(8,128)(2,1)S(1)} %get-tuple-element.27.refs_0_, bf16[160,1024]{1,0:T(8,128)(2,1)S(1)} %get-tuple-element.28.refs_1_, bf16[1,2,80,512]{3,2,1,0:T(8,128)(2,1)S(1)} %shard_map.63.refs_2_, ...), custom_call_target="tpu_custom_call" | custom-call | tf_op jit(solution)/shard_map/pallas_call | solution.py:156
  109.2 2.7 %shard_map.68 = (f32[1024,512]{1,0:T(8,128)S(1)}, f32[1024,512]{1,0:T(8,128)S(1)}, f32[5,8,128]{2,1,0:T(8,128)S(1)}) custom-call(s32[2]{0:T(128)S(1)} %pad_add_fusion.3.where, bf16[160,1024]{1,0:T(8,128)(2,1)S(1)} %collective-permute-done.8.refs_0_, bf16[160,1024]{1,0:T(8,128)(2,1)S(1)} %collective-permute-done.9.refs_1_, ...), custom_call_target="tpu_custom_call" | custom-call | tf_op jit(solution)/shard_map/pallas_call | solution.py:156
  111.9 3.2 %shard_map.72 = (f32[1024,512]{1,0:T(8,128)S(1)}, f32[1024,512]{1,0:T(8,128)S(1)}, f32[9,8,128]{2,1,0:T(8,128)S(1)}) custom-call(s32[2]{0:T(128)S(1)} %pad_add_fusion.3.where, bf16[160,1024]{1,0:T(8,128)(2,1)S(1)} %collective-permute-done.17.refs_0_, bf16[160,1024]{1,0:T(8,128)(2,1)S(1)} %collective-permute-done.18.refs_1_, ...), custom_call_target="tpu_custom_call" | custom-call | tf_op jit(solution)/shard_map/pallas_call | solution.py:156
  115.1 3.8 %shard_map.76 = (f32[1024,512]{1,0:T(8,128)S(1)}, f32[1024,512]{1,0:T(8,128)S(1)}, f32[13,8,128]{2,1,0:T(8,128)S(1)}) custom-call(s32[2]{0:T(128)S(1)} %pad_add_fusion.3.where, bf16[160,1024]{1,0:T(8,128)(2,1)S(1)} %collective-permute-done.26.refs_0_, bf16[160,1024]{1,0:T(8,128)(2,1)S(1)} %collective-permute-done.27.refs_1_, ...), custom_call_target="tpu_custom_call" | custom-call | tf_op jit(solution)/shard_map/pallas_call | solution.py:156
  118.9 2.6 %shard_map.80 = (f32[1024,512]{1,0:T(8,128)S(1)}, f32[8,8,128]{2,1,0:T(8,128)S(1)}) custom-call(s32[2]{0:T(128)S(1)} %pad_add_fusion.3.where, bf16[160,1024]{1,0:T(8,128)(2,1)S(1)} %collective-permute-done.35.refs_0_, bf16[160,1024]{1,0:T(8,128)(2,1)S(1)} %collective-permute-done.36.refs_1_, bf16[1,2,80,512]{3,2,1,0:T(8,128)(2,1)S(1)} %shard_map.79.refs_2_, ...), custom_call_target="tpu_custom_call" | custom-call | tf_op jit(solution)/shard_map/pallas_call | solution.py:156
  125.1 2.1 %collective-permute-done.42 = f32[8,128]{1,0:T(8,128)S(1)} collective-permute-done((f32[8,128]{1,0:T(8,128)S(1)}, f32[8,128]{1,0:T(8,128)S(1)}, u32[]{:S(2)}, u32[]{:S(2)}) %collective-permute-start.42) | collective-permute-done | bytes 4128 | tf_op jit(solution)/shard_map/ppermute | solution.py:321
  127.2 1.7 %collective-permute-start.43 = (f32[8,128]{1,0:T(8,128)S(1)}, f32[8,128]{1,0:T(8,128)S(1)}, u32[]{:S(2)}, u32[]{:S(2)}) collective-permute-start(f32[8,128]{1,0:T(8,128)S(1)} %add.16), channel_id=1, source_target_pairs={{0,4},{4,0},{8,12},{12,8},{16,20},{20,16},{24,28},{28,24},{1,5},{5... | collective-permute-start | bytes 12296 | tf_op jit(solution)/shard_map/ppermute | solution.py:324
  129.0 1.9 %collective-permute-done.43 = f32[8,128]{1,0:T(8,128)S(1)} collective-permute-done((f32[8,128]{1,0:T(8,128)S(1)}, f32[8,128]{1,0:T(8,128)S(1)}, u32[]{:S(2)}, u32[]{:S(2)}) %collective-permute-start.43) | collective-permute-done | bytes 4128 | tf_op jit(solution)/shard_map/ppermute | solution.py:324
  131.4 3.0 %collective-permute-done.44 = f32[8,128]{1,0:T(8,128)S(1)} collective-permute-done((f32[8,128]{1,0:T(8,128)S(1)}, f32[8,128]{1,0:T(8,128)S(1)}, u32[]{:S(2)}, u32[]{:S(2)}) %collective-permute-start.44) | collective-permute-done | bytes 4128 | tf_op jit(solution)/shard_map/ppermute | solution.py:324
  134.8 4.2 %collective-permute-done.45 = f32[8,128]{1,0:T(8,128)S(1)} collective-permute-done((f32[8,128]{1,0:T(8,128)S(1)}, f32[8,128]{1,0:T(8,128)S(1)}, u32[]{:S(2)}, u32[]{:S(2)}) %collective-permute-start.45) | collective-permute-done | bytes 4128 | tf_op jit(solution)/shard_map/ppermute | solution.py:324
  139.0 3.9 %combine.1 = (f32[1024,512]{1,0:T(8,128)}, f32[1024,512]{1,0:T(8,128)}) custom-call(s32[2]{0:T(128)S(1)} %pad_add_fusion.3.where, f32[8,128]{1,0:T(8,128)S(1)} %add.19.products, f32[1024,512]{1,0:T(8,128)S(1)} %copy-done.1, f32[1024,512]{1,0:T(8,128)S(1)} %get-tuple-element.34.refs_6_.refs_4_.refs_0_, ...), custom_call_target="tpu_custom_call" | custom-call | tf_op jit(solution)/shard_map/combine/pallas_call | solution.py:329
  (104 shorter events, 42.7 us)
Async XLA Ops:
  2.4 11.7 %collective-permute-start.10 = (bf16[160,1024]{1,0:T(8,128)(2,1)S(1)}, bf16[160,1024]{1,0:T(8,128)(2,1)S(1)}, u32[]{:S(2)}, u32[]{:S(2)}) collective-permute-start(bf16[160,1024]{1,0:T(8,128)(2,1)S(1)} %get-tuple-element.27.refs_0_), channel_id=1, source_target_pairs={{8,0},{16,8},{24,16},{28,24},{20,28},{12,20},{4,12},{0,4},{9,1},{1... | collective-permute-start | bytes 983048 | tf_op jit(solution)/shard_map/ppermute | solution.py:241
  5.4 10.6 %collective-permute-start.8 = (bf16[160,1024]{1,0:T(8,128)(2,1)S(1)}, bf16[160,1024]{1,0:T(8,128)(2,1)S(1)}, u32[]{:S(2)}, u32[]{:S(2)}) collective-permute-start(bf16[160,1024]{1,0:T(8,128)(2,1)S(1)} %get-tuple-element.27.refs_0_), channel_id=1, source_target_pairs={{0,8},{8,16},{16,24},{24,28},{28,20},{20,12},{12,4},{4,0},{1,9},{9... | collective-permute-start | bytes 983048 | tf_op jit(solution)/shard_map/ppermute | solution.py:238
  5.6 21.8 %collective-permute-start.11 = (bf16[160,1024]{1,0:T(8,128)(2,1)S(1)}, bf16[160,1024]{1,0:T(8,128)(2,1)S(1)}, u32[]{:S(2)}, u32[]{:S(2)}) collective-permute-start(bf16[160,1024]{1,0:T(8,128)(2,1)S(1)} %get-tuple-element.28.refs_1_), channel_id=1, source_target_pairs={{8,0},{16,8},{24,16},{28,24},{20,28},{12,20},{4,12},{0,4},{9,1},{1... | collective-permute-start | bytes 983048 | tf_op jit(solution)/shard_map/ppermute | solution.py:239
  7.4 13.1 %collective-permute-start.3 = (s32[1,80]{1,0:T(1,128)}, s32[1,80]{1,0:T(1,128)S(1)}, u32[]{:S(2)}, u32[]{:S(2)}) collective-permute-start(s32[1,80]{1,0:T(1,128)} %bitcast.3), channel_id=1, source_target_pairs={{0,4},{4,0},{8,12},{12,8},{16,20},{20,16},{24,28},{28,24},{1,5},{5... | collective-permute-start | bytes 968 | tf_op jit(solution)/shard_map/ppermute | solution.py:253
  9.0 21.3 %collective-permute-start.9 = (bf16[160,1024]{1,0:T(8,128)(2,1)S(1)}, bf16[160,1024]{1,0:T(8,128)(2,1)S(1)}, u32[]{:S(2)}, u32[]{:S(2)}) collective-permute-start(bf16[160,1024]{1,0:T(8,128)(2,1)S(1)} %get-tuple-element.28.refs_1_), channel_id=1, source_target_pairs={{0,8},{8,16},{16,24},{24,28},{28,20},{20,12},{12,4},{4,0},{1,9},{9... | collective-permute-start | bytes 983048 | tf_op jit(solution)/shard_map/ppermute | solution.py:240
  14.1 16.5 %collective-permute-start.19 = (bf16[160,1024]{1,0:T(8,128)(2,1)S(1)}, bf16[160,1024]{1,0:T(8,128)(2,1)S(1)}, u32[]{:S(2)}, u32[]{:S(2)}) collective-permute-start(bf16[160,1024]{1,0:T(8,128)(2,1)S(1)} %collective-permute-done.10.refs_1_.refs_2_), channel_id=1, source_target_pairs={{8,0},{16,8},{24,16},{28,24},{20,28},{12,20},{4,12},{0,4},{9,1},{1... | collective-permute-start | bytes 983048 | tf_op jit(solution)/shard_map/ppermute | solution.py:241
  16.0 14.5 %collective-permute-start.17 = (bf16[160,1024]{1,0:T(8,128)(2,1)S(1)}, bf16[160,1024]{1,0:T(8,128)(2,1)S(1)}, u32[]{:S(2)}, u32[]{:S(2)}) collective-permute-start(bf16[160,1024]{1,0:T(8,128)(2,1)S(1)} %collective-permute-done.8.refs_0_), channel_id=1, source_target_pairs={{0,8},{8,16},{16,24},{24,28},{28,20},{20,12},{12,4},{4,0},{1,9},{9... | collective-permute-start | bytes 983048 | tf_op jit(solution)/shard_map/ppermute | solution.py:238
  27.3 29.1 %collective-permute-start.1 = (bf16[1024,512]{1,0:T(8,128)(2,1)S(1)}, bf16[1024,512]{1,0:T(8,128)(2,1)S(1)}, u32[]{:S(2)}, u32[]{:S(2)}) collective-permute-start(bf16[1024,512]{1,0:T(8,128)(2,1)S(1)} %shard_map.60.refs_2_.refs_4_), channel_id=1, source_target_pairs={{0,1},{1,0},{2,3},{3,2},{4,5},{5,4},{6,7},{7,6},{8,9},{9,8},{10,11... | collective-permute-start | bytes 3145736 | tf_op jit(solution)/shard_map/ppermute | solution.py:277
  27.3 10.6 %collective-permute-start.20 = (bf16[160,1024]{1,0:T(8,128)(2,1)S(1)}, bf16[160,1024]{1,0:T(8,128)(2,1)S(1)}, u32[]{:S(2)}, u32[]{:S(2)}) collective-permute-start(bf16[160,1024]{1,0:T(8,128)(2,1)S(1)} %collective-permute-done.11.refs_3_), channel_id=1, source_target_pairs={{8,0},{16,8},{24,16},{28,24},{20,28},{12,20},{4,12},{0,4},{9,1},{1... | collective-permute-start | bytes 983048 | tf_op jit(solution)/shard_map/ppermute | solution.py:239
  30.3 10.1 %collective-permute-start.13 = (bf16[160,1024]{1,0:T(8,128)(2,1)S(1)}, bf16[160,1024]{1,0:T(8,128)(2,1)S(1)}, u32[]{:S(2)}, u32[]{:S(2)}) collective-permute-start(bf16[160,1024]{1,0:T(8,128)(2,1)S(1)} %collective-permute-done.11.refs_3_), channel_id=1, source_target_pairs={{0,1},{1,0},{2,3},{3,2},{4,5},{5,4},{6,7},{7,6},{8,9},{9,8},{10,11... | collective-permute-start | bytes 983048 | tf_op jit(solution)/shard_map/ppermute | solution.py:283
  30.5 9.9 %collective-permute-start.18 = (bf16[160,1024]{1,0:T(8,128)(2,1)S(1)}, bf16[160,1024]{1,0:T(8,128)(2,1)S(1)}, u32[]{:S(2)}, u32[]{:S(2)}) collective-permute-start(bf16[160,1024]{1,0:T(8,128)(2,1)S(1)} %collective-permute-done.9.refs_1_), channel_id=1, source_target_pairs={{0,8},{8,16},{16,24},{24,28},{28,20},{20,12},{12,4},{4,0},{1,9},{9... | collective-permute-start | bytes 983048 | tf_op jit(solution)/shard_map/ppermute | solution.py:240
  30.5 11.9 %collective-permute-start.12 = (bf16[160,1024]{1,0:T(8,128)(2,1)S(1)}, bf16[160,1024]{1,0:T(8,128)(2,1)S(1)}, u32[]{:S(2)}, u32[]{:S(2)}) collective-permute-start(bf16[160,1024]{1,0:T(8,128)(2,1)S(1)} %collective-permute-done.9.refs_1_), channel_id=1, source_target_pairs={{0,1},{1,0},{2,3},{3,2},{4,5},{5,4},{6,7},{7,6},{8,9},{9,8},{10,11... | collective-permute-start | bytes 983048 | tf_op jit(solution)/shard_map/ppermute | solution.py:283
  37.9 10.6 %collective-permute-start.28 = (bf16[160,1024]{1,0:T(8,128)(2,1)S(1)}, bf16[160,1024]{1,0:T(8,128)(2,1)S(1)}, u32[]{:S(2)}, u32[]{:S(2)}) collective-permute-start(bf16[160,1024]{1,0:T(8,128)(2,1)S(1)} %collective-permute-done.19.refs_1_.refs_2_), channel_id=1, source_target_pairs={{8,0},{16,8},{24,16},{28,24},{20,28},{12,20},{4,12},{0,4},{9,1},{1... | collective-permute-start | bytes 983048 | tf_op jit(solution)/shard_map/ppermute | solution.py:241
  40.4 10.6 %collective-permute-start.26 = (bf16[160,1024]{1,0:T(8,128)(2,1)S(1)}, bf16[160,1024]{1,0:T(8,128)(2,1)S(1)}, u32[]{:S(2)}, u32[]{:S(2)}) collective-permute-start(bf16[160,1024]{1,0:T(8,128)(2,1)S(1)} %collective-permute-done.17.refs_0_), channel_id=1, source_target_pairs={{0,8},{8,16},{16,24},{24,28},{28,20},{20,12},{12,4},{4,0},{1,9},{9... | collective-permute-start | bytes 983048 | tf_op jit(solution)/shard_map/ppermute | solution.py:238
  40.4 13.8 %collective-permute-start.29 = (bf16[160,1024]{1,0:T(8,128)(2,1)S(1)}, bf16[160,1024]{1,0:T(8,128)(2,1)S(1)}, u32[]{:S(2)}, u32[]{:S(2)}) collective-permute-start(bf16[160,1024]{1,0:T(8,128)(2,1)S(1)} %collective-permute-done.20.refs_3_), channel_id=1, source_target_pairs={{8,0},{16,8},{24,16},{28,24},{20,28},{12,20},{4,12},{0,4},{9,1},{1... | collective-permute-start | bytes 983048 | tf_op jit(solution)/shard_map/ppermute | solution.py:239
  42.4 14.0 %collective-permute-start.27 = (bf16[160,1024]{1,0:T(8,128)(2,1)S(1)}, bf16[160,1024]{1,0:T(8,128)(2,1)S(1)}, u32[]{:S(2)}, u32[]{:S(2)}) collective-permute-start(bf16[160,1024]{1,0:T(8,128)(2,1)S(1)} %collective-permute-done.18.refs_1_), channel_id=1, source_target_pairs={{0,8},{8,16},{16,24},{24,28},{28,20},{20,12},{12,4},{4,0},{1,9},{9... | collective-permute-start | bytes 983048 | tf_op jit(solution)/shard_map/ppermute | solution.py:240
  48.5 10.7 %collective-permute-start.22 = (bf16[160,1024]{1,0:T(8,128)(2,1)S(1)}, bf16[160,1024]{1,0:T(8,128)(2,1)S(1)}, u32[]{:S(2)}, u32[]{:S(2)}) collective-permute-start(bf16[160,1024]{1,0:T(8,128)(2,1)S(1)} %collective-permute-done.20.refs_3_), channel_id=1, source_target_pairs={{0,1},{1,0},{2,3},{3,2},{4,5},{5,4},{6,7},{7,6},{8,9},{9,8},{10,11... | collective-permute-start | bytes 983048 | tf_op jit(solution)/shard_map/ppermute | solution.py:283
  51.0 9.9 %collective-permute-start.21 = (bf16[160,1024]{1,0:T(8,128)(2,1)S(1)}, bf16[160,1024]{1,0:T(8,128)(2,1)S(1)}, u32[]{:S(2)}, u32[]{:S(2)}) collective-permute-start(bf16[160,1024]{1,0:T(8,128)(2,1)S(1)} %collective-permute-done.18.refs_1_), channel_id=1, source_target_pairs={{0,1},{1,0},{2,3},{3,2},{4,5},{5,4},{6,7},{7,6},{8,9},{9,8},{10,11... | collective-permute-start | bytes 983048 | tf_op jit(solution)/shard_map/ppermute | solution.py:283
  56.4 10.2 %collective-permute-start.36 = (bf16[160,1024]{1,0:T(8,128)(2,1)S(1)}, bf16[160,1024]{1,0:T(8,128)(2,1)S(1)}, u32[]{:S(2)}, u32[]{:S(2)}) collective-permute-start(bf16[160,1024]{1,0:T(8,128)(2,1)S(1)} %collective-permute-done.29.refs_3_), channel_id=1, source_target_pairs={{8,0},{16,8},{24,16},{28,24},{20,28},{12,20},{4,12},{0,4},{9,1},{1... | collective-permute-start | bytes 983048 | tf_op jit(solution)/shard_map/ppermute | solution.py:239
  59.2 10.6 %collective-permute-start.14 = (f32[2,80,512]{2,1,0:T(8,128)S(1)}, f32[2,80,512]{2,1,0:T(8,128)S(1)}, u32[]{:S(2)}, u32[]{:S(2)}) collective-permute-start(f32[2,80,512]{2,1,0:T(8,128)S(1)} %get-tuple-element.33), channel_id=1, source_target_pairs={{0,2},{1,3},{2,0},{3,1},{4,6},{5,7},{6,4},{7,5},{8,10},{9,11},{10,... | collective-permute-start | bytes 983048 | tf_op jit(solution)/shard_map/ppermute | solution.py:287
  62.7 14.2 %collective-permute-start.23 = (f32[2,80,512]{2,1,0:T(8,128)S(1)}, f32[2,80,512]{2,1,0:T(8,128)S(1)}, u32[]{:S(2)}, u32[]{:S(2)}) collective-permute-start(f32[2,80,512]{2,1,0:T(8,128)S(1)} %get-tuple-element.37), channel_id=1, source_target_pairs={{0,2},{1,3},{2,0},{3,1},{4,6},{5,7},{6,4},{7,5},{8,10},{9,11},{10,... | collective-permute-start | bytes 983048 | tf_op jit(solution)/shard_map/ppermute | solution.py:287
  64.7 19.2 %collective-permute-start.32 = (f32[2,80,512]{2,1,0:T(8,128)S(1)}, f32[2,80,512]{2,1,0:T(8,128)S(1)}, u32[]{:S(2)}, u32[]{:S(2)}) collective-permute-start(f32[2,80,512]{2,1,0:T(8,128)S(1)} %get-tuple-element.42), channel_id=1, source_target_pairs={{0,2},{1,3},{2,0},{3,1},{4,6},{5,7},{6,4},{7,5},{8,10},{9,11},{10,... | collective-permute-start | bytes 983048 | tf_op jit(solution)/shard_map/ppermute | solution.py:287
  66.4 19.6 %collective-permute-start = (bf16[160,1024]{1,0:T(8,128)(2,1)S(1)}, bf16[160,1024]{1,0:T(8,128)(2,1)S(1)}, u32[]{:S(2)}, u32[]{:S(2)}) collective-permute-start(bf16[160,1024]{1,0:T(8,128)(2,1)S(1)} %get-tuple-element.28.refs_1_), channel_id=1, source_target_pairs={{0,1},{1,0},{2,3},{3,2},{4,5},{5,4},{6,7},{7,6},{8,9},{9,8},{10,11... | collective-permute-start | bytes 983048 | tf_op jit(solution)/shard_map/ppermute | solution.py:283
  66.6 21.1 %collective-permute-start.35 = (bf16[160,1024]{1,0:T(8,128)(2,1)S(1)}, bf16[160,1024]{1,0:T(8,128)(2,1)S(1)}, u32[]{:S(2)}, u32[]{:S(2)}) collective-permute-start(bf16[160,1024]{1,0:T(8,128)(2,1)S(1)} %collective-permute-done.26.refs_0_), channel_id=1, source_target_pairs={{0,8},{8,16},{16,24},{24,28},{28,20},{20,12},{12,4},{4,0},{1,9},{9... | collective-permute-start | bytes 983048 | tf_op jit(solution)/shard_map/ppermute | solution.py:238
  69.9 19.4 %collective-permute-start.37 = (bf16[160,1024]{1,0:T(8,128)(2,1)S(1)}, bf16[160,1024]{1,0:T(8,128)(2,1)S(1)}, u32[]{:S(2)}, u32[]{:S(2)}) collective-permute-start(bf16[160,1024]{1,0:T(8,128)(2,1)S(1)} %collective-permute-done.36.refs_1_), channel_id=1, source_target_pairs={{0,1},{1,0},{2,3},{3,2},{4,5},{5,4},{6,7},{7,6},{8,9},{9,8},{10,11... | collective-permute-start | bytes 983048 | tf_op jit(solution)/shard_map/ppermute | solution.py:283
  76.9 14.0 %collective-permute-start.15 = (bf16[2,80,512]{2,1,0:T(8,128)(2,1)S(1)}, bf16[2,80,512]{2,1,0:T(8,128)(2,1)S(1)}, u32[]{:S(2)}, u32[]{:S(2)}) collective-permute-start(bf16[2,80,512]{2,1,0:T(8,128)(2,1)S(1)} %shard_map.66.mine), channel_id=1, source_target_pairs={{0,2},{1,3},{2,0},{3,1},{4,6},{5,7},{6,4},{7,5},{8,10},{9,11},{10,... | collective-permute-start | bytes 491528 | tf_op jit(solution)/shard_map/ppermute | solution.py:296
  87.7 10.3 %collective-permute-start.2 = (f32[1,80,512]{2,1,0:T(8,128)S(1)}, f32[1,80,512]{2,1,0:T(8,128)S(1)}, u32[]{:S(2)}, u32[]{:S(2)}) collective-permute-start(f32[1,80,512]{2,1,0:T(8,128)S(1)} %get-tuple-element.30), channel_id=1, source_target_pairs={{0,2},{1,3},{2,0},{3,1},{4,6},{5,7},{6,4},{7,5},{8,10},{9,11},{10,... | collective-permute-start | bytes 491528 | tf_op jit(solution)/shard_map/ppermute | solution.py:287
  90.4 11.2 %collective-permute-start.38 = (f32[1,80,512]{2,1,0:T(8,128)S(1)}, f32[1,80,512]{2,1,0:T(8,128)S(1)}, u32[]{:S(2)}, u32[]{:S(2)}) collective-permute-start(f32[1,80,512]{2,1,0:T(8,128)S(1)} %get-tuple-element.47), channel_id=1, source_target_pairs={{0,2},{1,3},{2,0},{3,1},{4,6},{5,7},{6,4},{7,5},{8,10},{9,11},{10,... | collective-permute-start | bytes 491528 | tf_op jit(solution)/shard_map/ppermute | solution.py:287
  91.5 17.6 %collective-permute-start.16 = (bf16[2,2,80,512]{3,2,1,0:T(8,128)(2,1)S(1)}, bf16[2,2,80,512]{3,2,1,0:T(8,128)(2,1)S(1)}, u32[]{:S(2)}, u32[]{:S(2)}) collective-permute-start(bf16[2,2,80,512]{3,2,1,0:T(8,128)(2,1)S(1)} %shard_map.67.refs_4_), channel_id=1, source_target_pairs={{0,1},{1,0},{2,3},{3,2},{4,5},{5,4},{6,7},{7,6},{8,9},{9,8},{10,11... | collective-permute-start | bytes 983048 | tf_op jit(solution)/shard_map/ppermute | solution.py:298
  92.2 19.6 %collective-permute-start.25 = (bf16[2,2,80,512]{3,2,1,0:T(8,128)(2,1)S(1)}, bf16[2,2,80,512]{3,2,1,0:T(8,128)(2,1)S(1)}, u32[]{:S(2)}, u32[]{:S(2)}) collective-permute-start(bf16[2,2,80,512]{3,2,1,0:T(8,128)(2,1)S(1)} %shard_map.71.refs_4_), channel_id=1, source_target_pairs={{0,1},{1,0},{2,3},{3,2},{4,5},{5,4},{6,7},{7,6},{8,9},{9,8},{10,11... | collective-permute-start | bytes 983048 | tf_op jit(solution)/shard_map/ppermute | solution.py:298
  95.1 20.0 %collective-permute-start.34 = (bf16[2,2,80,512]{3,2,1,0:T(8,128)(2,1)S(1)}, bf16[2,2,80,512]{3,2,1,0:T(8,128)(2,1)S(1)}, u32[]{:S(2)}, u32[]{:S(2)}) collective-permute-start(bf16[2,2,80,512]{3,2,1,0:T(8,128)(2,1)S(1)} %shard_map.75.refs_4_), channel_id=1, source_target_pairs={{0,1},{1,0},{2,3},{3,2},{4,5},{5,4},{6,7},{7,6},{8,9},{9,8},{10,11... | collective-permute-start | bytes 983048 | tf_op jit(solution)/shard_map/ppermute | solution.py:298
  107.2 11.7 %collective-permute-start.40 = (bf16[1,2,80,512]{3,2,1,0:T(8,128)(2,1)S(1)}, bf16[1,2,80,512]{3,2,1,0:T(8,128)(2,1)S(1)}, u32[]{:S(2)}, u32[]{:S(2)}) collective-permute-start(bf16[1,2,80,512]{3,2,1,0:T(8,128)(2,1)S(1)} %shard_map.79.refs_2_), channel_id=1, source_target_pairs={{0,1},{1,0},{2,3},{3,2},{4,5},{5,4},{6,7},{7,6},{8,9},{9,8},{10,11... | collective-permute-start | bytes 491528 | tf_op jit(solution)/shard_map/ppermute | solution.py:298
  (19 other events, 139.8 us)
where the time goes:
time: 143 us
  waiting for transfers between devices  66.1 us (46%)
  starting transfers between devices  39.1 us (27%)
  Pallas kernels  33.2 us (23%)
  local copies, waits for them, and re-layouts  2.69 us (2%)
    pallas_call x23, Pallas kernels, local_call(): pl.pallas_call(kernel, in_specs=[pl.BlockSpec(memory_space=pltpu.SMEM)] +...  28.2 us
    ppermute x5, waiting for transfers between devices, ring_path(): got = lax.ppermute(send, 'shard', swap_y)  17.1 us
    ppermute x4, waiting for transfers between devices, ring_path(): d = lax.ppermute(from_right[-1][1], 'rep', left)  10.4 us
    ppermute x3, waiting for transfers between devices, ring_path(): c = None if last else lax.ppermute(from_right[-1][0], 'rep', left)  9.47 us
    ppermute x3, waiting for transfers between devices, ring_path(): lax.ppermute(products, 'rep', [(i, i ^ bit) for i in range(count)])  9.03 us
    ppermute x3, waiting for transfers between devices, ring_path(): lax.ppermute(all_targets, 'rep', pairs)  8.39 us
    ppermute x4, starting transfers between devices, ring_path(): d = lax.ppermute(from_right[-1][1], 'rep', left)  8.26 us
    ppermute x3, starting transfers between devices, ring_path(): c = None if last else lax.ppermute(from_right[-1][0], 'rep', left)  7.43 us
  transfers between devices with their start and end apart: 46, of which 22 were waited for; matrix products, arithmetic and copies ran while one was open for 0% of the time, Pallas kernels for 18%

commit v1 on v0

v1 whole, which is shorter than its diff:
```python
import functools

import jax
import jax.numpy as jnp
from jax import lax
from jax.experimental import pallas as pl
from jax.experimental.pallas import tpu as pltpu
from jax.sharding import PartitionSpec as P


epsilon = 1e-06
step_size = 0.05


def mix_pair(cross, norm_low, norm_high):
    norm_low = jnp.maximum(norm_low, 0.0)
    norm_high = jnp.maximum(norm_high, 0.0)
    bound = jnp.sqrt(norm_low) * jnp.sqrt(norm_high)
    cross = jnp.minimum(jnp.maximum(cross, -bound), bound)
    return (
        1.0 - cross / (2.0 * (norm_low + epsilon)),
        1.0 - cross / (2.0 * (norm_high + epsilon)),
    )


def tree_weights(entry, count):
    products = {(a, b): entry(a, b) for a in range(count) for b in range(a, count)}
    weights = [None] * count
    group = 1
    alive = count
    while alive > 1:
        factors = []
        for m in range(alive // 2):
            low, high = mix_pair(
                products[2 * m, 2 * m + 1], products[2 * m, 2 * m], products[2 * m + 1, 2 * m + 1]
            )
            factors.append((low, high))
            for r in range(2 * m * group, (2 * m + 1) * group):
                weights[r] = low if weights[r] is None else weights[r] * low
            for r in range((2 * m + 1) * group, (2 * m + 2) * group):
                weights[r] = high if weights[r] is None else weights[r] * high
        merged = {}
        for a in range(alive // 2):
            for b in range(a, alive // 2):
                terms = [
                    factors[a][i]
                    * factors[b][j]
                    * products[min(2 * a + i, 2 * b + j), max(2 * a + i, 2 * b + j)]
                    for i in range(2)
                    for j in range(2)
                ]
                merged[a, b] = (terms[0] + terms[3]) + (terms[1] + terms[2])
        products = merged
        alive //= 2
        group *= 2
    return weights


def grad_kernel(where, *refs, blocks, phases, olds):
    news = len(blocks)
    xs = refs[: 2 * news]
    errors = refs[2 * news : 2 * news + 4 * phases]
    old = refs[2 * news + 4 * phases : 2 * news + 4 * phases + olds]
    new = refs[2 * news + 4 * phases + olds : 3 * news + 4 * phases + olds]
    sums = refs[-1]
    second = where[1] & 1 == 1
    upper = where[1] >> 1 == 1
    for n, ends in enumerate(blocks):
        parts = []
        for half, (phase, slot) in enumerate(ends):
            mine, across, other, other_across = [ref[slot] for ref in errors[4 * phase : 4 * phase + 4]]
            if half:
                here, there = jnp.where(upper, mine, across), jnp.where(upper, other, other_across)
            else:
                here, there = jnp.where(upper, across, mine), jnp.where(upper, other_across, other)
            parts += [jnp.where(second, there, here), jnp.where(second, here, there)]
        new[n][...] = lax.dot_general(
            jnp.concatenate([xs[2 * n][...], xs[2 * n + 1][...]], axis=0),
            jnp.concatenate(parts, axis=0),
            (((0,), (0,)), ((), ())),
            preferred_element_type=jnp.float32,
        )
    every = list(old) + list(new)
    pairs = [(i, olds + n) for n in range(news) for i in range(olds + n + 1)]
    features, columns = new[0].shape

    def body(step, carry):
        carry = list(carry)
        for c in range(columns // 128):
            got = [ref[pl.ds(pl.multiple_of(step * 8, 8), 8), c * 128 : (c + 1) * 128] for ref in every]
            for k, (i, j) in enumerate(pairs):
                carry[k] = carry[k] + got[i] * got[j]
        return tuple(carry)

    totals = lax.fori_loop(
        0, features // 8, body, tuple(jnp.zeros((8, 128), jnp.float32) for _ in pairs), unroll=4
    )
    for k in range(len(pairs)):
        sums[k] = totals[k]


def ring_replica(index, count):
    return jnp.where(index < count // 2, 2 * index, 2 * (count - 1 - index) + 1)


def ring_place(replica, count):
    return jnp.where(replica % 2 == 0, replica // 2, count - 1 - replica // 2)


def replica_at(rep, offset, count):
    index = ring_place(rep, count) + offset % count
    return ring_replica(jnp.where(index >= count, index - count, index), count)


def place_kernel(where, *refs, pairs, offsets):
    out = refs[-1]
    count = len(offsets)
    ids = [replica_at(where[0], offset, count) for offset in offsets]
    row = lax.broadcasted_iota(jnp.int32, (8, 128), 0)
    column = lax.broadcasted_iota(jnp.int32, (8, 128), 1)
    tile = jnp.zeros((8, 128), jnp.float32)
    at = 0
    for ref in refs[:-1]:
        for k in range(ref.shape[0]):
            i, j = pairs[at]
            at += 1
            total = jnp.sum(ref[k], axis=(0, 1), keepdims=True)
            here = ((row == ids[i]) & (column == ids[j])) | ((row == ids[j]) & (column == ids[i]))
            tile = jnp.where(here, total, tile)
    out[...] = tile


def combine_kernel(where, products, weight, *refs, offsets, parts):
    count = len(offsets)
    grads = refs[:count]
    combined, new_weight, made, moved, sems = refs[count:]
    weights = tree_weights(lambda a, b: jnp.full((8, 128), products[a, b], jnp.float32), count)
    local = []
    for offset in offsets:
        mine = replica_at(where[0], offset, count)
        value = weights[0]
        for a in range(1, count):
            value = jnp.where(mine == a, weights[a], value)
        local.append(value)
    features, columns = made.shape
    tile = features // parts

    def copies(part):
        rows = pl.ds(part * tile, tile)
        return (
            pltpu.make_async_copy(made.at[rows], combined.at[rows], sems.at[0, part]),
            pltpu.make_async_copy(moved.at[rows], new_weight.at[rows], sems.at[1, part]),
        )

    for part in range(parts):

        def body(step, carry):
            rows = pl.ds(pl.multiple_of(part * tile + step * 8, 8), 8)
            for c in range(columns // 128):
                lanes = slice(c * 128, (c + 1) * 128)
                total = local[0] * grads[0][rows, lanes]
                for i in range(1, count):
                    total = total + local[i] * grads[i][rows, lanes]
                made[rows, lanes] = total
                moved[rows, lanes] = weight[rows, lanes] - step_size * total
            return carry

        lax.fori_loop(0, tile // 8, body, 0, unroll=4)
        for copy in copies(part):
            copy.start()
    for part in range(parts):
        for copy in copies(part):
            copy.wait()


def local_call(kernel, shapes, *args):
    vmem = pl.BlockSpec(memory_space=pltpu.VMEM)
    out = pl.pallas_call(
        kernel,
        in_specs=[pl.BlockSpec(memory_space=pltpu.SMEM)] + [vmem] * (len(args) - 1),
        out_specs=[vmem] * len(shapes),
        out_shape=[jax.ShapeDtypeStruct(shape, dtype) for shape, dtype in shapes],
        compiler_params=pltpu.CompilerParams(vmem_limit_bytes=12 * 2**20),
    )(*args)
    return out


def cast_kernel(where, weight, weight_b):
    weight_b[...] = weight[...].astype(weight_b.dtype)


def rows_of(core, quarter):
    return pl.ds(pl.multiple_of(core * quarter, quarter), quarter)


def pick_kernel(where, *refs):
    out = refs[-1]
    theirs = rows_of(1 - (where[1] & 1), out.shape[1])
    for n in range(out.shape[0]):
        out[n] = refs[n][theirs]


def join_kernel(where, *refs):
    refs[-1][...] = jnp.concatenate([ref[...] for ref in refs[:-1]])


def outputs_kernel(where, *refs):
    weight_b, weight_other, keep, send = refs[-4:]
    slots, quarter = keep.shape[:2]
    xs = refs[: 2 * slots]
    got = refs[2 * slots : -4]
    upper = where[1] >> 1 == 1
    rows = rows_of(where[1] & 1, quarter)
    for n in range(slots):
        mine = jnp.concatenate([xs[2 * n + half][rows] for half in range(2)])
        if len(got) == 1:
            other = jnp.concatenate([got[0][2 * n + half] for half in range(2)])
        else:
            other = jnp.concatenate([got[2 * n + half][rows] for half in range(2)])
        made = jnp.dot(mine, weight_b[...], preferred_element_type=jnp.float32)
        made += jnp.dot(other, weight_other[...], preferred_element_type=jnp.float32)
        first, second = made[:quarter], made[quarter:]
        keep[n] = jnp.where(upper, second, first)
        send[n] = jnp.where(upper, first, second)


def error_kernel(where, *refs, at, rows):
    wanted, error = refs[-2:]
    n = 0
    for mine, got in zip(refs[:-2:2], refs[1:-2:2]):
        for slot in range(mine.shape[0]):
            error[n] = ((mine[slot] + got[slot] - wanted[at + n]) / rows).astype(error.dtype)
            n += 1


def wanted_kernel(where, *refs, slots):
    table, wanted = refs[-2:]
    count = len(slots)
    targets = [ref[k : k + 1] for ref in refs[:-2] for k in range(ref.shape[0])]
    candidates = lax.broadcasted_iota(jnp.int32, (table.shape[0], wanted.shape[1]), 0)
    for i, (first, second) in enumerate(slots):
        offset = jnp.where(where[1] >> 1 == 1, second % count, first % count)
        place = replica_at(where[0], offset, count) ^ where[0]
        chosen = targets[0]
        for k in range(1, count):
            chosen = jnp.where(place == k, targets[k], chosen)
        hot = (candidates == chosen).astype(table.dtype)
        wanted[i] = lax.dot_general(
            hot, table[...], (((0,), (0,)), ((), ())), preferred_element_type=jnp.float32
        )


def ring_path(inputs, weight, table, targets):
    count = lax.axis_size("rep")
    rows = inputs.shape[0]
    features, columns = weight.shape
    quarter = rows // 4
    right = []
    left = []
    for i in range(count):
        ends = [2 * r if r < count // 2 else 2 * (count - 1 - r) + 1 for r in (i, (i + 1) % count)]
        right.append((ends[0], ends[1]))
        left.append((ends[1], ends[0]))
    far = count // 2
    where = jnp.stack([lax.axis_index("rep"), lax.axis_index("shard")])

    from_left = [[inputs[: rows // 2], inputs[rows // 2 :]]]
    from_right = [from_left[0]]
    for step in range(1, far + 1):
        last = step == far
        a = lax.ppermute(from_left[-1][0], "rep", right)
        d = lax.ppermute(from_right[-1][1], "rep", left)
        b = None if last else lax.ppermute(from_left[-1][1], "rep", right)
        c = None if last else lax.ppermute(from_right[-1][0], "rep", left)
        from_left.append([a, b])
        from_right.append([c, d])
    halves = {0: from_left[0], far: [from_left[far][0], from_right[far][1]]}
    for step in range(1, far):
        halves[-step] = from_left[step]
        halves[step] = from_right[step]
    phases = [[(0, 0)]]
    phases += [[(-step, step), (step, -step)] for step in range(1, far - 1)]
    phases += [[(1 - far, far - 1)], [(far - 1, 1 - far)], [(far, far)]]
    slots = tuple(slot for phase in phases for slot in phase)
    joined = [[0, 1]] + [[m] for m in range(2, far - 1)] + [[far - 1, far], [far + 1]]
    groups = [[0, -1, 1]] + [[-step, step] for step in range(2, far)] + [[far]]
    offsets = tuple(offset for group in groups for offset in group)

    pieces = [targets[None]]
    for i in range(count.bit_length() - 1):
        block = pieces[0]
        if i:
            shape = ((1 << i, quarter), targets.dtype)
            (block,) = local_call(join_kernel, (shape,), where, *pieces)
        pieces.append(lax.ppermute(block, "rep", [(r, r ^ 1 << i) for r in range(count)]))
    wanted = pl.pallas_call(
        functools.partial(wanted_kernel, slots=slots),
        grid_spec=pltpu.PrefetchScalarGridSpec(
            num_scalar_prefetch=1,
            grid=(1,),
            in_specs=[pl.BlockSpec(piece.shape, lambda i, where: (0, 0)) for piece in pieces]
            + [pl.BlockSpec((table.shape[0], columns), lambda i, where: (0, where[0]))],
            out_specs=pl.BlockSpec((count, quarter, columns), lambda i, where: (0, 0, 0)),
        ),
        out_shape=jax.ShapeDtypeStruct((count, quarter, columns), jnp.float32),
        compiler_params=pltpu.CompilerParams(vmem_limit_bytes=8 * 2**20),
        name="wanted",
    )(where, *pieces, table)

    swap_core = [(i, i ^ 1) for i in range(4)]
    swap_y = [(i, i ^ 2) for i in range(4)]
    (weight_b,) = local_call(cast_kernel, ((weight.shape, jnp.bfloat16),), where, weight)
    weight_other = lax.ppermute(weight_b, "shard", swap_core)
    summed = []
    for phase in phases:
        part = ((len(phase), quarter, columns), jnp.float32)
        xs = [halves[slot[half]][half] for slot in phase for half in range(2)]
        outgoing = xs
        if len(phase) > 1:
            shape = ((len(xs), quarter, features), inputs.dtype)
            outgoing = local_call(pick_kernel, (shape,), where, *xs)
        others = [lax.ppermute(x, "shard", swap_core) for x in outgoing]
        keep, send = local_call(outputs_kernel, (part, part), where, *xs, *others, weight_b, weight_other)
        summed += [(keep, lax.ppermute(send, "shard", swap_y))]

    errors = []
    errors_at = {}
    at = 0
    for m, members in enumerate(joined):
        mine = [slot for phase in members for slot in phases[phase]]
        for n, ends in enumerate(mine):
            errors_at[ends[0], 0] = (m, n)
            errors_at[ends[1], 1] = (m, n)
        (error,) = local_call(
            functools.partial(error_kernel, at=at, rows=rows),
            (((len(mine), quarter, columns), jnp.bfloat16),),
            where,
            *[part for phase in members for part in summed[phase]],
            wanted,
        )
        across = lax.ppermute(error, "shard", swap_y)
        other = lax.ppermute(error, "shard", swap_core)
        errors.append((error, across, other, lax.ppermute(across, "shard", swap_core)))
        at += len(mine)

    grads = []
    sums = []
    pairs = []
    for group in groups:
        olds = len(grads)
        needed = sorted({errors_at[offset, half][0] for offset in group for half in range(2)})
        blocks = tuple(
            tuple((needed.index(errors_at[offset, half][0]), errors_at[offset, half][1]) for half in range(2))
            for offset in group
        )
        fresh = [(i, olds + n) for n in range(len(group)) for i in range(olds + n + 1)]
        made = local_call(
            functools.partial(grad_kernel, blocks=blocks, phases=len(needed), olds=olds),
            ((weight.shape, jnp.float32),) * len(group) + (((len(fresh), 8, 128), jnp.float32),),
            where,
            *[halves[offset][half] for offset in group for half in range(2)],
            *[part for phase in needed for part in errors[phase]],
            *grads,
        )
        pairs += fresh
        grads = grads + list(made[: len(group)])
        sums.append(made[len(group)])

    (products,) = local_call(
        functools.partial(place_kernel, pairs=pairs, offsets=offsets), (((8, 128), jnp.float32),), where, *sums
    )
    products = products + lax.ppermute(products, "shard", swap_core)
    products = products + lax.ppermute(products, "shard", swap_y)
    bit = 1
    while bit < count:
        products = products + lax.ppermute(products, "rep", [(i, i ^ bit) for i in range(count)])
        bit *= 2
    parts = 8
    smem = pl.BlockSpec(memory_space=pltpu.SMEM)
    vmem = pl.BlockSpec(memory_space=pltpu.VMEM)
    block = jax.ShapeDtypeStruct((features, columns), jnp.float32)
    return pl.pallas_call(
        functools.partial(combine_kernel, offsets=offsets, parts=parts),
        in_specs=[smem, smem] + [vmem] * (1 + count),
        out_specs=[pl.BlockSpec(memory_space=pltpu.HBM)] * 2,
        out_shape=[block] * 2,
        scratch_shapes=[pltpu.VMEM(block.shape, block.dtype)] * 2 + [pltpu.SemaphoreType.DMA((2, parts))],
        compiler_params=pltpu.CompilerParams(vmem_limit_bytes=12 * 2**20),
        name="combine",
    )(where, products, weight, *grads)


def gather_path(inputs, weight, table, targets):
    count = lax.axis_size("rep")
    rows = inputs.shape[0]
    features, columns = weight.shape
    rep = lax.axis_index("rep")
    all_inputs = lax.all_gather(inputs, "rep", axis=0, tiled=True)
    all_targets = lax.all_gather(targets, "rep", axis=0, tiled=False)
    partial = jnp.dot(all_inputs, weight.astype(jnp.bfloat16), preferred_element_type=jnp.float32)
    outputs = lax.psum_scatter(
        partial.reshape(count, rows, columns), "shard", scatter_dimension=1, tiled=True
    )
    table_columns = lax.dynamic_slice(table, (0, rep * columns), (table.shape[0], columns))
    wanted = table_columns[all_targets].astype(jnp.float32)
    error = ((outputs - wanted) / rows).astype(jnp.bfloat16)
    errors = lax.all_gather(error, "shard", axis=1, tiled=True)
    grads = lax.dot_general(
        all_inputs.reshape(count, rows, features),
        errors,
        (((1,), (1,)), ((0,), (0,))),
        preferred_element_type=jnp.float32,
    )
    products = lax.dot_general(
        grads, grads, (((1, 2), (1, 2)), ((), ())), precision=lax.Precision.HIGHEST
    )
    products = lax.psum(products, ("rep", "shard"))
    weights = jnp.stack(tree_weights(lambda a, b: products[a, b], count))
    combined = jnp.sum(weights[:, None, None] * grads, axis=0)
    return combined, weight - step_size * combined


def solution(mesh):
    count, shards = mesh.shape["rep"], mesh.shape["shard"]
    ring = shards == 4 and count == 8

    def on_device(inputs, weight, table, targets):
        if ring:
            return tuple(ring_path(inputs, weight, table, targets))
        return gather_path(inputs, weight, table, targets)

    in_specs = (P("rep", "shard"), P("shard", "rep"), P(), P(("rep", "shard")))
    out_specs = (P("shard", "rep"), P("shard", "rep"))
    return jax.shard_map(
        on_device, mesh=mesh, in_specs=in_specs, out_specs=out_specs, check_vma=False
    )
```

time: 143 us -> 151 us (1.056)
  waiting for transfers between devices: 66.1 us -> 79.9 us
  Pallas kernels: 33.2 us -> 30.2 us
  starting transfers between devices: 39.1 us -> 36.3 us
    ppermute x26 -> x31, waiting for transfers between devices: 29.5 us -> 42.2 us  [the longest x6 17.9 us: ring_path(): summed += [(keep, lax.ppermute(send, 'shard', swap_y))]]
    ppermute x3, starting transfers between devices: 7.43 us -> 2.53 us  [ring_path(): c = None if last else lax.ppermute(from_right[-1][0], 'rep', left)]
    ppermute x4, starting transfers between devices: 0.94 us -> 5.79 us  [ring_path(): a = lax.ppermute(from_left[-1][0], 'rep', right)]
    ppermute x4, starting transfers between devices: 8.26 us -> 3.6 us  [ring_path(): d = lax.ppermute(from_right[-1][1], 'rep', left)]
    pallas_call x23 -> x20, Pallas kernels: 28.2 us -> 26 us  [local_call(): pl.pallas_call(kernel, in_specs=[pl.BlockSpec(memory_space=pltpu.SMEM)] +...]
    ppermute x3, waiting for transfers between devices: 9.47 us -> 11.6 us  [ring_path(): c = None if last else lax.ppermute(from_right[-1][0], 'rep', left)]
    ppermute x26 -> x31, starting transfers between devices: 16.1 us -> 17.7 us  [the longest x6 7.28 us: ring_path(): summed += [(keep, lax.ppermute(send, 'shard', swap_y))]]
  transfers between devices with their start and end apart: 46 -> 51, of which waited for: 22 -> 22; matrix products, arithmetic and copies ran while one was open for 0% -> 0% of each run, Pallas kernels for 18% -> 16%
where the time goes in v1:
time: 151 us
  waiting for transfers between devices  79.9 us (53%)
  starting transfers between devices  36.3 us (24%)
  Pallas kernels  30.2 us (20%)
  local copies, waits for them, and re-layouts  3.37 us (2%)
    pallas_call x20, Pallas kernels, local_call(): pl.pallas_call(kernel, in_specs=[pl.BlockSpec(memory_space=pltpu.SMEM)] +...  26 us
    ppermute x6, waiting for transfers between devices, ring_path(): summed += [(keep, lax.ppermute(send, 'shard', swap_y))]  17.9 us
    ppermute x3, waiting for transfers between devices, ring_path(): lax.ppermute(block, 'rep', [(r, r ^ 1 << i) for r in range(count)])  14.9 us
    ppermute x3, waiting for transfers between devices, ring_path(): c = None if last else lax.ppermute(from_right[-1][0], 'rep', left)  11.6 us
    ppermute x4, waiting for transfers between devices, ring_path(): d = lax.ppermute(from_right[-1][1], 'rep', left)  9.46 us
    ppermute x4, waiting for transfers between devices, ring_path(): across = lax.ppermute(error, 'shard', swap_y)  9.35 us
    ppermute x3, waiting for transfers between devices, ring_path(): lax.ppermute(products, 'rep', [(i, i ^ bit) for i in range(count)])  9.19 us
    ppermute x6, starting transfers between devices, ring_path(): summed += [(keep, lax.ppermute(send, 'shard', swap_y))]  7.28 us
  transfers between devices with their start and end apart: 51, of which 22 were waited for; matrix products, arithmetic and copies ran while one was open for 0% of the time, Pallas kernels for 16%

profile of v1, /device:TPU:0, one launch (start us, length us, event | category | flops | bytes accessed | tf_op | source)
XLA Modules:
  0.0 151.0 jit_solution(5024908280875822098)
XLA Ops:
  2.3 2.5 %collective-permute-start.3 = (bf16[160,1024]{1,0:T(8,128)(2,1)S(1)}, bf16[160,1024]{1,0:T(8,128)(2,1)S(1)}, u32[]{:S(2)}, u32[]{:S(2)}) collective-permute-start(bf16[160,1024]{1,0:T(8,128)(2,1)S(1)} %get-tuple-element.50.refs_1_), channel_id=1, source_target_pairs={{8,0},{16,8},{24,16},{28,24},{20,28},{12,20},{4,12},{0,4},{9,1},{1... | collective-permute-start | bytes 983048 | tf_op jit(solution)/shard_map/ppermute | solution.py:272
  5.1 1.8 %collective-permute-start.10 = (s32[1,80]{1,0:T(1,128)}, s32[1,80]{1,0:T(1,128)S(1)}, u32[]{:S(2)}, u32[]{:S(2)}) collective-permute-start(s32[1,80]{1,0:T(1,128)} %bitcast.3), channel_id=1, source_target_pairs={{0,4},{4,0},{8,12},{12,8},{16,20},{20,16},{24,28},{28,24},{1,5},{5... | collective-permute-start | bytes 968 | tf_op jit(solution)/shard_map/ppermute | solution.py:295
  7.0 7.8 %collective-permute-done.10.refs_1_ = s32[1,80]{1,0:T(1,128)S(1)} collective-permute-done((s32[1,80]{1,0:T(1,128)}, s32[1,80]{1,0:T(1,128)S(1)}, u32[]{:S(2)}, u32[]{:S(2)}) %collective-permute-start.10) | collective-permute-done | bytes 352 | tf_op jit(solution)/shard_map/ppermute | solution.py:295
  16.0 3.6 %collective-permute-done.11.refs_2_ = s32[2,80]{1,0:T(2,128)S(1)} collective-permute-done((s32[2,80]{1,0:T(2,128)S(1)}, s32[2,80]{1,0:T(2,128)S(1)}, u32[]{:S(2)}, u32[]{:S(2)}) %collective-permute-start.11) | collective-permute-done | bytes 672 | tf_op jit(solution)/shard_map/ppermute | solution.py:295
  21.1 3.6 %collective-permute-done.12.refs_3_ = s32[4,80]{1,0:T(4,128)S(1)} collective-permute-done((s32[4,80]{1,0:T(4,128)S(1)}, s32[4,80]{1,0:T(4,128)S(1)}, u32[]{:S(2)}, u32[]{:S(2)}) %collective-permute-start.12) | collective-permute-done | bytes 1312 | tf_op jit(solution)/shard_map/ppermute | solution.py:295
  25.0 1.8 %collective-permute-start = (bf16[160,1024]{1,0:T(8,128)(2,1)S(1)}, bf16[160,1024]{1,0:T(8,128)(2,1)S(1)}, u32[]{:S(2)}, u32[]{:S(2)}) collective-permute-start(bf16[160,1024]{1,0:T(8,128)(2,1)S(1)} %get-tuple-element.51.refs_0_), channel_id=1, source_target_pairs={{0,8},{8,16},{16,24},{24,28},{28,20},{20,12},{12,4},{4,0},{1,9},{9... | collective-permute-start | bytes 983048 | tf_op jit(solution)/shard_map/ppermute | solution.py:271
  27.0 1.8 %collective-permute-start.17 = (bf16[160,1024]{1,0:T(8,128)(2,1)S(1)}, bf16[160,1024]{1,0:T(8,128)(2,1)S(1)}, u32[]{:S(2)}, u32[]{:S(2)}) collective-permute-start(bf16[160,1024]{1,0:T(8,128)(2,1)S(1)} %collective-permute-done.1.refs_3_), channel_id=1, source_target_pairs={{0,8},{8,16},{16,24},{24,28},{28,20},{20,12},{12,4},{4,0},{1,9},{9... | collective-permute-start | bytes 983048 | tf_op jit(solution)/shard_map/ppermute | solution.py:273
  28.8 1.6 %copy-done = f32[1024,512]{1,0:T(8,128)S(1)} copy-done((f32[1024,512]{1,0:T(8,128)S(1)}, f32[1024,512]{1,0:T(8,128)}, u32[]{:S(2)}) %copy-start) | copy-done | bytes 2097176
  31.1 4.2 %collective-permute-done.2.refs_2_.refs_4_ = bf16[160,1024]{1,0:T(8,128)(2,1)S(1)} collective-permute-done((bf16[160,1024]{1,0:T(8,128)(2,1)S(1)}, bf16[160,1024]{1,0:T(8,128)(2,1)S(1)}, u32[]{:S(2)}, u32[]{:S(2)}) %collective-permute-start.2) | collective-permute-done | bytes 327712 | tf_op jit(solution)/shard_map/ppermute | solution.py:274
  35.5 1.8 %collective-permute-start.16 = (bf16[160,1024]{1,0:T(8,128)(2,1)S(1)}, bf16[160,1024]{1,0:T(8,128)(2,1)S(1)}, u32[]{:S(2)}, u32[]{:S(2)}) collective-permute-start(bf16[160,1024]{1,0:T(8,128)(2,1)S(1)} %collective-permute-done.refs_0_.refs_2_), channel_id=1, source_target_pairs={{0,8},{8,16},{16,24},{24,28},{28,20},{20,12},{12,4},{4,0},{1,9},{9... | collective-permute-start | bytes 983048 | tf_op jit(solution)/shard_map/ppermute | solution.py:271
  37.3 5.0 %collective-permute-done.19.refs_1_.refs_3_ = bf16[160,1024]{1,0:T(8,128)(2,1)S(1)} collective-permute-done((bf16[160,1024]{1,0:T(8,128)(2,1)S(1)}, bf16[160,1024]{1,0:T(8,128)(2,1)S(1)}, u32[]{:S(2)}, u32[]{:S(2)}) %collective-permute-start.19) | collective-permute-done | bytes 327712 | tf_op jit(solution)/shard_map/ppermute | solution.py:272
  43.2 6.1 %collective-permute-done.18.refs_2_ = bf16[160,1024]{1,0:T(8,128)(2,1)S(1)} collective-permute-done((bf16[160,1024]{1,0:T(8,128)(2,1)S(1)}, bf16[160,1024]{1,0:T(8,128)(2,1)S(1)}, u32[]{:S(2)}, u32[]{:S(2)}) %collective-permute-start.18) | collective-permute-done | bytes 327712 | tf_op jit(solution)/shard_map/ppermute | solution.py:274
  49.3 2.0 %collective-permute-start.27 = (bf16[160,1024]{1,0:T(8,128)(2,1)S(1)}, bf16[160,1024]{1,0:T(8,128)(2,1)S(1)}, u32[]{:S(2)}, u32[]{:S(2)}) collective-permute-start(bf16[160,1024]{1,0:T(8,128)(2,1)S(1)} %collective-permute-done.18.refs_2_), channel_id=1, source_target_pairs={{8,0},{16,8},{24,16},{28,24},{20,28},{12,20},{4,12},{0,4},{9,1},{1... | collective-permute-start | bytes 983048 | tf_op jit(solution)/shard_map/ppermute | solution.py:274
  51.3 4.5 %collective-permute-done.28.refs_1_.refs_3_ = bf16[160,1024]{1,0:T(8,128)(2,1)S(1)} collective-permute-done((bf16[160,1024]{1,0:T(8,128)(2,1)S(1)}, bf16[160,1024]{1,0:T(8,128)(2,1)S(1)}, u32[]{:S(2)}, u32[]{:S(2)}) %collective-permute-start.28) | collective-permute-done | bytes 327712 | tf_op jit(solution)/shard_map/ppermute | solution.py:272
  59.3 3.6 %collective-permute-done.25.refs_0_ = bf16[160,1024]{1,0:T(8,128)(2,1)S(1)} collective-permute-done((bf16[160,1024]{1,0:T(8,128)(2,1)S(1)}, bf16[160,1024]{1,0:T(8,128)(2,1)S(1)}, u32[]{:S(2)}, u32[]{:S(2)}) %collective-permute-start.25) | collective-permute-done | bytes 327712 | tf_op jit(solution)/shard_map/ppermute | solution.py:271
  65.4 1.7 %collective-permute-start.38 = (bf16[160,1024]{1,0:T(8,128)(2,1)S(1)}, bf16[160,1024]{1,0:T(8,128)(2,1)S(1)}, u32[]{:S(2)}, u32[]{:S(2)}) collective-permute-start(bf16[160,1024]{1,0:T(8,128)(2,1)S(1)} %collective-permute-done.25.refs_0_), channel_id=1, source_target_pairs={{0,8},{8,16},{16,24},{24,28},{28,20},{20,12},{12,4},{4,0},{1,9},{9... | collective-permute-start | bytes 983048 | tf_op jit(solution)/shard_map/ppermute | solution.py:271
  72.5 7.7 %collective-permute-done.7.refs_1_ = f32[1,80,512]{2,1,0:T(8,128)S(1)} collective-permute-done((f32[1,80,512]{2,1,0:T(8,128)S(1)}, f32[1,80,512]{2,1,0:T(8,128)S(1)}, u32[]{:S(2)}, u32[]{:S(2)}) %collective-permute-start.7) | collective-permute-done | bytes 163872 | tf_op jit(solution)/shard_map/ppermute | solution.py:324
  88.8 2.0 %collective-permute-done.31.refs_1_ = f32[1,80,512]{2,1,0:T(8,128)S(1)} collective-permute-done((f32[1,80,512]{2,1,0:T(8,128)S(1)}, f32[1,80,512]{2,1,0:T(8,128)S(1)}, u32[]{:S(2)}, u32[]{:S(2)}) %collective-permute-start.31) | collective-permute-done | bytes 163872 | tf_op jit(solution)/shard_map/ppermute | solution.py:324
  91.3 6.4 %collective-permute-done.21.refs_1_ = f32[2,80,512]{2,1,0:T(8,128)S(1)} collective-permute-done((f32[2,80,512]{2,1,0:T(8,128)S(1)}, f32[2,80,512]{2,1,0:T(8,128)S(1)}, u32[]{:S(2)}, u32[]{:S(2)}) %collective-permute-start.21) | collective-permute-done | bytes 327712 | tf_op jit(solution)/shard_map/ppermute | solution.py:324
  103.6 2.9 %collective-permute-done.22.refs_5_ = bf16[2,80,512]{2,1,0:T(8,128)(2,1)S(1)} collective-permute-done((bf16[2,80,512]{2,1,0:T(8,128)(2,1)S(1)}, bf16[2,80,512]{2,1,0:T(8,128)(2,1)S(1)}, u32[]{:S(2)}, u32[]{:S(2)}) %collective-permute-start.22) | collective-permute-done | bytes 163872 | tf_op jit(solution)/shard_map/ppermute | solution.py:341
  106.5 3.3 %collective-permute-done.35.refs_5_ = bf16[2,80,512]{2,1,0:T(8,128)(2,1)S(1)} collective-permute-done((bf16[2,80,512]{2,1,0:T(8,128)(2,1)S(1)}, bf16[2,80,512]{2,1,0:T(8,128)(2,1)S(1)}, u32[]{:S(2)}, u32[]{:S(2)}) %collective-permute-start.35) | collective-permute-done | bytes 163872 | tf_op jit(solution)/shard_map/ppermute | solution.py:341
  109.9 1.8 %collective-permute-done.42.refs_1_ = f32[1,80,512]{2,1,0:T(8,128)S(1)} collective-permute-done((f32[1,80,512]{2,1,0:T(8,128)S(1)}, f32[1,80,512]{2,1,0:T(8,128)S(1)}, u32[]{:S(2)}, u32[]{:S(2)}) %collective-permute-start.42) | collective-permute-done | bytes 163872 | tf_op jit(solution)/shard_map/ppermute | solution.py:324
  114.0 3.1 %collective-permute-done.43.refs_3_ = bf16[1,80,512]{2,1,0:T(8,128)(2,1)S(1)} collective-permute-done((bf16[1,80,512]{2,1,0:T(8,128)(2,1)S(1)}, bf16[1,80,512]{2,1,0:T(8,128)(2,1)S(1)}, u32[]{:S(2)}, u32[]{:S(2)}) %collective-permute-start.43) | collective-permute-done | bytes 81952 | tf_op jit(solution)/shard_map/ppermute | solution.py:341
  117.1 3.3 %shard_map.66 = (f32[1024,512]{1,0:T(8,128)S(1)}, f32[1024,512]{1,0:T(8,128)S(1)}, f32[1024,512]{1,0:T(8,128)S(1)}, f32[6,8,128]{2,1,0:T(8,128)S(1)}) custom-call(s32[2]{0:T(128)S(1)} %pad_add_fusion.where, bf16[160,1024]{1,0:T(8,128)(2,1)S(1)} %get-tuple-element.51.refs_0_, bf16[160,1024]{1,0:T(8,128)(2,1)S(1)} %get-tuple-element.50.refs_1_, ...), custom_call_target="tpu_custom_call" | custom-call | tf_op jit(solution)/shard_map/pallas_call | solution.py:178
  120.5 3.2 %shard_map.70 = (f32[1024,512]{1,0:T(8,128)S(1)}, f32[1024,512]{1,0:T(8,128)S(1)}, f32[9,8,128]{2,1,0:T(8,128)S(1)}) custom-call(s32[2]{0:T(128)S(1)} %pad_add_fusion.where, bf16[160,1024]{1,0:T(8,128)(2,1)S(1)} %collective-permute-done.16.refs_0_, bf16[160,1024]{1,0:T(8,128)(2,1)S(1)} %collective-permute-done.17.refs_3_.refs_1_, ...), custom_call_target="tpu_custom_call" | custom-call | tf_op jit(solution)/shard_map/pallas_call | solution.py:178
  123.7 3.8 %shard_map.74 = (f32[1024,512]{1,0:T(8,128)S(1)}, f32[1024,512]{1,0:T(8,128)S(1)}, f32[13,8,128]{2,1,0:T(8,128)S(1)}) custom-call(s32[2]{0:T(128)S(1)} %pad_add_fusion.where, bf16[160,1024]{1,0:T(8,128)(2,1)S(1)} %collective-permute-done.25.refs_0_, bf16[160,1024]{1,0:T(8,128)(2,1)S(1)} %collective-permute-done.26.refs_1_, ...), custom_call_target="tpu_custom_call" | custom-call | tf_op jit(solution)/shard_map/pallas_call | solution.py:178
  127.6 2.6 %shard_map.77 = (f32[1024,512]{1,0:T(8,128)S(1)}, f32[8,8,128]{2,1,0:T(8,128)S(1)}) custom-call(s32[2]{0:T(128)S(1)} %pad_add_fusion.where, bf16[160,1024]{1,0:T(8,128)(2,1)S(1)} %collective-permute-done.38.refs_0_, bf16[160,1024]{1,0:T(8,128)(2,1)S(1)} %collective-permute-done.39.refs_1_, bf16[1,80,512]{2,1,0:T(8,128)(2,1)S(1)} %shard_map.76.refs_2_, ...), custom_call_target="tpu_custom_call" | custom-call | tf_op jit(solution)/shard_map/pallas_call | solution.py:178
  133.8 2.1 %collective-permute-done.47 = f32[8,128]{1,0:T(8,128)S(1)} collective-permute-done((f32[8,128]{1,0:T(8,128)S(1)}, f32[8,128]{1,0:T(8,128)S(1)}, u32[]{:S(2)}, u32[]{:S(2)}) %collective-permute-start.47) | collective-permute-done | bytes 4128 | tf_op jit(solution)/shard_map/ppermute | solution.py:373
  136.4 3.1 %collective-permute-done.48 = f32[8,128]{1,0:T(8,128)S(1)} collective-permute-done((f32[8,128]{1,0:T(8,128)S(1)}, f32[8,128]{1,0:T(8,128)S(1)}, u32[]{:S(2)}, u32[]{:S(2)}) %collective-permute-start.48) | collective-permute-done | bytes 4128 | tf_op jit(solution)/shard_map/ppermute | solution.py:376
  140.1 3.1 %collective-permute-done.49 = f32[8,128]{1,0:T(8,128)S(1)} collective-permute-done((f32[8,128]{1,0:T(8,128)S(1)}, f32[8,128]{1,0:T(8,128)S(1)}, u32[]{:S(2)}, u32[]{:S(2)}) %collective-permute-start.49) | collective-permute-done | bytes 4128 | tf_op jit(solution)/shard_map/ppermute | solution.py:376
  144.6 3.0 %collective-permute-done.50 = f32[8,128]{1,0:T(8,128)S(1)} collective-permute-done((f32[8,128]{1,0:T(8,128)S(1)}, f32[8,128]{1,0:T(8,128)S(1)}, u32[]{:S(2)}, u32[]{:S(2)}) %collective-permute-start.50) | collective-permute-done | bytes 4128 | tf_op jit(solution)/shard_map/ppermute | solution.py:376
  147.7 3.2 %combine.1 = (f32[1024,512]{1,0:T(8,128)}, f32[1024,512]{1,0:T(8,128)}) custom-call(s32[2]{0:T(128)S(1)} %pad_add_fusion.where, f32[8,128]{1,0:T(8,128)S(1)} %add.19.products, f32[1024,512]{1,0:T(8,128)S(1)} %copy-done.1, f32[1024,512]{1,0:T(8,128)S(1)} %get-tuple-element.33.refs_8_.refs_6_.refs_0_, ...), custom_call_target="tpu_custom_call" | custom-call | tf_op jit(solution)/shard_map/combine/pallas_call | solution.py:382
  (107 shorter events, 42.2 us)
Async XLA Ops:
  1.7 23.2 %collective-permute-start.5 = (bf16[160,1024]{1,0:T(8,128)(2,1)S(1)}, bf16[160,1024]{1,0:T(8,128)(2,1)S(1)}, u32[]{:S(2)}, u32[]{:S(2)}) collective-permute-start(bf16[160,1024]{1,0:T(8,128)(2,1)S(1)} %get-tuple-element.50.refs_1_), channel_id=1, source_target_pairs={{0,1},{1,0},{2,3},{3,2},{4,5},{5,4},{6,7},{7,6},{8,9},{9,8},{10,11... | collective-permute-start | bytes 983048 | tf_op jit(solution)/shard_map/ppermute | solution.py:322
  2.3 24.4 %collective-permute-start.3 = (bf16[160,1024]{1,0:T(8,128)(2,1)S(1)}, bf16[160,1024]{1,0:T(8,128)(2,1)S(1)}, u32[]{:S(2)}, u32[]{:S(2)}) collective-permute-start(bf16[160,1024]{1,0:T(8,128)(2,1)S(1)} %get-tuple-element.50.refs_1_), channel_id=1, source_target_pairs={{8,0},{16,8},{24,16},{28,24},{20,28},{12,20},{4,12},{0,4},{9,1},{1... | collective-permute-start | bytes 983048 | tf_op jit(solution)/shard_map/ppermute | solution.py:272
  4.8 22.1 %collective-permute-start.1 = (bf16[160,1024]{1,0:T(8,128)(2,1)S(1)}, bf16[160,1024]{1,0:T(8,128)(2,1)S(1)}, u32[]{:S(2)}, u32[]{:S(2)}) collective-permute-start(bf16[160,1024]{1,0:T(8,128)(2,1)S(1)} %get-tuple-element.50.refs_1_), channel_id=1, source_target_pairs={{0,8},{8,16},{16,24},{24,28},{28,20},{20,12},{12,4},{4,0},{1,9},{9... | collective-permute-start | bytes 983048 | tf_op jit(solution)/shard_map/ppermute | solution.py:273
  5.0 26.0 %collective-permute-start.4 = (bf16[160,1024]{1,0:T(8,128)(2,1)S(1)}, bf16[160,1024]{1,0:T(8,128)(2,1)S(1)}, u32[]{:S(2)}, u32[]{:S(2)}) collective-permute-start(bf16[160,1024]{1,0:T(8,128)(2,1)S(1)} %get-tuple-element.51.refs_0_), channel_id=1, source_target_pairs={{0,1},{1,0},{2,3},{3,2},{4,5},{5,4},{6,7},{7,6},{8,9},{9,8},{10,11... | collective-permute-start | bytes 983048 | tf_op jit(solution)/shard_map/ppermute | solution.py:322
  24.7 10.6 %collective-permute-start.2 = (bf16[160,1024]{1,0:T(8,128)(2,1)S(1)}, bf16[160,1024]{1,0:T(8,128)(2,1)S(1)}, u32[]{:S(2)}, u32[]{:S(2)}) collective-permute-start(bf16[160,1024]{1,0:T(8,128)(2,1)S(1)} %get-tuple-element.51.refs_0_), channel_id=1, source_target_pairs={{8,0},{16,8},{24,16},{28,24},{20,28},{12,20},{4,12},{0,4},{9,1},{1... | collective-permute-start | bytes 983048 | tf_op jit(solution)/shard_map/ppermute | solution.py:274
  25.0 10.6 %collective-permute-start = (bf16[160,1024]{1,0:T(8,128)(2,1)S(1)}, bf16[160,1024]{1,0:T(8,128)(2,1)S(1)}, u32[]{:S(2)}, u32[]{:S(2)}) collective-permute-start(bf16[160,1024]{1,0:T(8,128)(2,1)S(1)} %get-tuple-element.51.refs_0_), channel_id=1, source_target_pairs={{0,8},{8,16},{16,24},{24,28},{28,20},{20,12},{12,4},{4,0},{1,9},{9... | collective-permute-start | bytes 983048 | tf_op jit(solution)/shard_map/ppermute | solution.py:271
  26.7 15.6 %collective-permute-start.19 = (bf16[160,1024]{1,0:T(8,128)(2,1)S(1)}, bf16[160,1024]{1,0:T(8,128)(2,1)S(1)}, u32[]{:S(2)}, u32[]{:S(2)}) collective-permute-start(bf16[160,1024]{1,0:T(8,128)(2,1)S(1)} %collective-permute-done.3.refs_1_.refs_5_), channel_id=1, source_target_pairs={{8,0},{16,8},{24,16},{28,24},{20,28},{12,20},{4,12},{0,4},{9,1},{1... | collective-permute-start | bytes 983048 | tf_op jit(solution)/shard_map/ppermute | solution.py:272
  27.0 16.2 %collective-permute-start.17 = (bf16[160,1024]{1,0:T(8,128)(2,1)S(1)}, bf16[160,1024]{1,0:T(8,128)(2,1)S(1)}, u32[]{:S(2)}, u32[]{:S(2)}) collective-permute-start(bf16[160,1024]{1,0:T(8,128)(2,1)S(1)} %collective-permute-done.1.refs_3_), channel_id=1, source_target_pairs={{0,8},{8,16},{16,24},{24,28},{28,20},{20,12},{12,4},{4,0},{1,9},{9... | collective-permute-start | bytes 983048 | tf_op jit(solution)/shard_map/ppermute | solution.py:273
  31.0 32.4 %collective-permute-start.6 = (bf16[1024,512]{1,0:T(8,128)(2,1)S(1)}, bf16[1024,512]{1,0:T(8,128)(2,1)S(1)}, u32[]{:S(2)}, u32[]{:S(2)}) collective-permute-start(bf16[1024,512]{1,0:T(8,128)(2,1)S(1)} %shard_map.59.refs_4_.refs_5_), channel_id=1, source_target_pairs={{0,1},{1,0},{2,3},{3,2},{4,5},{5,4},{6,7},{7,6},{8,9},{9,8},{10,11... | collective-permute-start | bytes 3145736 | tf_op jit(solution)/shard_map/ppermute | solution.py:313
  35.3 14.0 %collective-permute-start.18 = (bf16[160,1024]{1,0:T(8,128)(2,1)S(1)}, bf16[160,1024]{1,0:T(8,128)(2,1)S(1)}, u32[]{:S(2)}, u32[]{:S(2)}) collective-permute-start(bf16[160,1024]{1,0:T(8,128)(2,1)S(1)} %collective-permute-done.2.refs_2_.refs_4_), channel_id=1, source_target_pairs={{8,0},{16,8},{24,16},{28,24},{20,28},{12,20},{4,12},{0,4},{9,1},{1... | collective-permute-start | bytes 983048 | tf_op jit(solution)/shard_map/ppermute | solution.py:274
  35.5 13.8 %collective-permute-start.16 = (bf16[160,1024]{1,0:T(8,128)(2,1)S(1)}, bf16[160,1024]{1,0:T(8,128)(2,1)S(1)}, u32[]{:S(2)}, u32[]{:S(2)}) collective-permute-start(bf16[160,1024]{1,0:T(8,128)(2,1)S(1)} %collective-permute-done.refs_0_.refs_2_), channel_id=1, source_target_pairs={{0,8},{8,16},{16,24},{24,28},{28,20},{20,12},{12,4},{4,0},{1,9},{9... | collective-permute-start | bytes 983048 | tf_op jit(solution)/shard_map/ppermute | solution.py:271
  42.3 13.5 %collective-permute-start.28 = (bf16[160,1024]{1,0:T(8,128)(2,1)S(1)}, bf16[160,1024]{1,0:T(8,128)(2,1)S(1)}, u32[]{:S(2)}, u32[]{:S(2)}) collective-permute-start(bf16[160,1024]{1,0:T(8,128)(2,1)S(1)} %collective-permute-done.19.refs_1_.refs_3_), channel_id=1, source_target_pairs={{8,0},{16,8},{24,16},{28,24},{20,28},{12,20},{4,12},{0,4},{9,1},{1... | collective-permute-start | bytes 983048 | tf_op jit(solution)/shard_map/ppermute | solution.py:272
  43.2 19.7 %collective-permute-start.8 = (bf16[4,80,1024]{2,1,0:T(8,128)(2,1)S(1)}, bf16[4,80,1024]{2,1,0:T(8,128)(2,1)S(1)}, u32[]{:S(2)}, u32[]{:S(2)}) collective-permute-start(bf16[4,80,1024]{2,1,0:T(8,128)(2,1)S(1)} %shard_map.61), channel_id=1, source_target_pairs={{0,1},{1,0},{2,3},{3,2},{4,5},{5,4},{6,7},{7,6},{8,9},{9,8},{10,11... | collective-permute-start | bytes 1966088 | tf_op jit(solution)/shard_map/ppermute | solution.py:322
  49.3 10.0 %collective-permute-start.27 = (bf16[160,1024]{1,0:T(8,128)(2,1)S(1)}, bf16[160,1024]{1,0:T(8,128)(2,1)S(1)}, u32[]{:S(2)}, u32[]{:S(2)}) collective-permute-start(bf16[160,1024]{1,0:T(8,128)(2,1)S(1)} %collective-permute-done.18.refs_2_), channel_id=1, source_target_pairs={{8,0},{16,8},{24,16},{28,24},{20,28},{12,20},{4,12},{0,4},{9,1},{1... | collective-permute-start | bytes 983048 | tf_op jit(solution)/shard_map/ppermute | solution.py:274
  58.0 23.7 %collective-permute-start.20 = (bf16[4,80,1024]{2,1,0:T(8,128)(2,1)S(1)}, bf16[4,80,1024]{2,1,0:T(8,128)(2,1)S(1)}, u32[]{:S(2)}, u32[]{:S(2)}) collective-permute-start(bf16[4,80,1024]{2,1,0:T(8,128)(2,1)S(1)} %shard_map.67), channel_id=1, source_target_pairs={{0,1},{1,0},{2,3},{3,2},{4,5},{5,4},{6,7},{7,6},{8,9},{9,8},{10,11... | collective-permute-start | bytes 1966088 | tf_op jit(solution)/shard_map/ppermute | solution.py:322
  63.5 20.1 %collective-permute-start.39 = (bf16[160,1024]{1,0:T(8,128)(2,1)S(1)}, bf16[160,1024]{1,0:T(8,128)(2,1)S(1)}, u32[]{:S(2)}, u32[]{:S(2)}) collective-permute-start(bf16[160,1024]{1,0:T(8,128)(2,1)S(1)} %collective-permute-done.28.refs_1_.refs_3_), channel_id=1, source_target_pairs={{8,0},{16,8},{24,16},{28,24},{20,28},{12,20},{4,12},{0,4},{9,1},{1... | collective-permute-start | bytes 983048 | tf_op jit(solution)/shard_map/ppermute | solution.py:272
  65.4 19.8 %collective-permute-start.38 = (bf16[160,1024]{1,0:T(8,128)(2,1)S(1)}, bf16[160,1024]{1,0:T(8,128)(2,1)S(1)}, u32[]{:S(2)}, u32[]{:S(2)}) collective-permute-start(bf16[160,1024]{1,0:T(8,128)(2,1)S(1)} %collective-permute-done.25.refs_0_), channel_id=1, source_target_pairs={{0,8},{8,16},{16,24},{24,28},{28,20},{20,12},{12,4},{4,0},{1,9},{9... | collective-permute-start | bytes 983048 | tf_op jit(solution)/shard_map/ppermute | solution.py:271
  67.2 18.0 %collective-permute-start.9 = (f32[2,80,512]{2,1,0:T(8,128)S(1)}, f32[2,80,512]{2,1,0:T(8,128)S(1)}, u32[]{:S(2)}, u32[]{:S(2)}) collective-permute-start(f32[2,80,512]{2,1,0:T(8,128)S(1)} %get-tuple-element.29), channel_id=1, source_target_pairs={{0,2},{1,3},{2,0},{3,1},{4,6},{5,7},{6,4},{7,5},{8,10},{9,11},{10,... | collective-permute-start | bytes 983048 | tf_op jit(solution)/shard_map/ppermute | solution.py:324
  69.8 10.4 %collective-permute-start.7 = (f32[1,80,512]{2,1,0:T(8,128)S(1)}, f32[1,80,512]{2,1,0:T(8,128)S(1)}, u32[]{:S(2)}, u32[]{:S(2)}) collective-permute-start(f32[1,80,512]{2,1,0:T(8,128)S(1)} %get-tuple-element.27), channel_id=1, source_target_pairs={{0,2},{1,3},{2,0},{3,1},{4,6},{5,7},{6,4},{7,5},{8,10},{9,11},{10,... | collective-permute-start | bytes 491528 | tf_op jit(solution)/shard_map/ppermute | solution.py:324
  83.6 14.2 %collective-permute-start.21 = (f32[2,80,512]{2,1,0:T(8,128)S(1)}, f32[2,80,512]{2,1,0:T(8,128)S(1)}, u32[]{:S(2)}, u32[]{:S(2)}) collective-permute-start(f32[2,80,512]{2,1,0:T(8,128)S(1)} %get-tuple-element.32), channel_id=1, source_target_pairs={{0,2},{1,3},{2,0},{3,1},{4,6},{5,7},{6,4},{7,5},{8,10},{9,11},{10,... | collective-permute-start | bytes 983048 | tf_op jit(solution)/shard_map/ppermute | solution.py:324
  85.2 14.8 %collective-permute-start.41 = (bf16[160,1024]{1,0:T(8,128)(2,1)S(1)}, bf16[160,1024]{1,0:T(8,128)(2,1)S(1)}, u32[]{:S(2)}, u32[]{:S(2)}) collective-permute-start(bf16[160,1024]{1,0:T(8,128)(2,1)S(1)} %collective-permute-done.39.refs_1_), channel_id=1, source_target_pairs={{0,1},{1,0},{2,3},{3,2},{4,5},{5,4},{6,7},{7,6},{8,9},{9,8},{10,11... | collective-permute-start | bytes 983048 | tf_op jit(solution)/shard_map/ppermute | solution.py:322
  85.2 15.3 %collective-permute-start.40 = (bf16[160,1024]{1,0:T(8,128)(2,1)S(1)}, bf16[160,1024]{1,0:T(8,128)(2,1)S(1)}, u32[]{:S(2)}, u32[]{:S(2)}) collective-permute-start(bf16[160,1024]{1,0:T(8,128)(2,1)S(1)} %collective-permute-done.38.refs_0_), channel_id=1, source_target_pairs={{0,1},{1,0},{2,3},{3,2},{4,5},{5,4},{6,7},{7,6},{8,9},{9,8},{10,11... | collective-permute-start | bytes 983048 | tf_op jit(solution)/shard_map/ppermute | solution.py:322
  87.4 15.7 %collective-permute-start.13 = (bf16[3,80,512]{2,1,0:T(8,128)(2,1)S(1)}, bf16[3,80,512]{2,1,0:T(8,128)(2,1)S(1)}, u32[]{:S(2)}, u32[]{:S(2)}) collective-permute-start(bf16[3,80,512]{2,1,0:T(8,128)(2,1)S(1)} %shard_map.65.refs_6_), channel_id=1, source_target_pairs={{0,2},{1,3},{2,0},{3,1},{4,6},{5,7},{6,4},{7,5},{8,10},{9,11},{10,... | collective-permute-start | bytes 737288 | tf_op jit(solution)/shard_map/ppermute | solution.py:341
  90.7 12.4 %collective-permute-start.14 = (bf16[3,80,512]{2,1,0:T(8,128)(2,1)S(1)}, bf16[3,80,512]{2,1,0:T(8,128)(2,1)S(1)}, u32[]{:S(2)}, u32[]{:S(2)}) collective-permute-start(bf16[3,80,512]{2,1,0:T(8,128)(2,1)S(1)} %shard_map.65.refs_6_), channel_id=1, source_target_pairs={{0,1},{1,0},{2,3},{3,2},{4,5},{5,4},{6,7},{7,6},{8,9},{9,8},{10,11... | collective-permute-start | bytes 737288 | tf_op jit(solution)/shard_map/ppermute | solution.py:342
  99.9 9.9 %collective-permute-start.35 = (bf16[2,80,512]{2,1,0:T(8,128)(2,1)S(1)}, bf16[2,80,512]{2,1,0:T(8,128)(2,1)S(1)}, u32[]{:S(2)}, u32[]{:S(2)}) collective-permute-start(bf16[2,80,512]{2,1,0:T(8,128)(2,1)S(1)} %shard_map.73.refs_4_), channel_id=1, source_target_pairs={{0,2},{1,3},{2,0},{3,1},{4,6},{5,7},{6,4},{7,5},{8,10},{9,11},{10,... | collective-permute-start | bytes 491528 | tf_op jit(solution)/shard_map/ppermute | solution.py:341
  101.5 10.1 %collective-permute-start.42 = (f32[1,80,512]{2,1,0:T(8,128)S(1)}, f32[1,80,512]{2,1,0:T(8,128)S(1)}, u32[]{:S(2)}, u32[]{:S(2)}) collective-permute-start(f32[1,80,512]{2,1,0:T(8,128)S(1)} %get-tuple-element.45), channel_id=1, source_target_pairs={{0,2},{1,3},{2,0},{3,1},{4,6},{5,7},{6,4},{7,5},{8,10},{9,11},{10,... | collective-permute-start | bytes 491528 | tf_op jit(solution)/shard_map/ppermute | solution.py:324
  103.1 10.7 %collective-permute-start.15 = (bf16[3,80,512]{2,1,0:T(8,128)(2,1)S(1)}, bf16[3,80,512]{2,1,0:T(8,128)(2,1)S(1)}, u32[]{:S(2)}, u32[]{:S(2)}) collective-permute-start(bf16[3,80,512]{2,1,0:T(8,128)(2,1)S(1)} %collective-permute-done.13.refs_7_), channel_id=1, source_target_pairs={{0,1},{1,0},{2,3},{3,2},{4,5},{5,4},{6,7},{7,6},{8,9},{9,8},{10,11... | collective-permute-start | bytes 737288 | tf_op jit(solution)/shard_map/ppermute | solution.py:343
  106.5 13.9 %collective-permute-start.24 = (bf16[2,80,512]{2,1,0:T(8,128)(2,1)S(1)}, bf16[2,80,512]{2,1,0:T(8,128)(2,1)S(1)}, u32[]{:S(2)}, u32[]{:S(2)}) collective-permute-start(bf16[2,80,512]{2,1,0:T(8,128)(2,1)S(1)} %collective-permute-done.22.refs_5_), channel_id=1, source_target_pairs={{0,1},{1,0},{2,3},{3,2},{4,5},{5,4},{6,7},{7,6},{8,9},{9,8},{10,11... | collective-permute-start | bytes 491528 | tf_op jit(solution)/shard_map/ppermute | solution.py:343
  109.9 13.9 %collective-permute-start.36 = (bf16[2,80,512]{2,1,0:T(8,128)(2,1)S(1)}, bf16[2,80,512]{2,1,0:T(8,128)(2,1)S(1)}, u32[]{:S(2)}, u32[]{:S(2)}) collective-permute-start(bf16[2,80,512]{2,1,0:T(8,128)(2,1)S(1)} %shard_map.73.refs_4_), channel_id=1, source_target_pairs={{0,1},{1,0},{2,3},{3,2},{4,5},{5,4},{6,7},{7,6},{8,9},{9,8},{10,11... | collective-permute-start | bytes 491528 | tf_op jit(solution)/shard_map/ppermute | solution.py:342
  111.6 12.1 %collective-permute-start.37 = (bf16[2,80,512]{2,1,0:T(8,128)(2,1)S(1)}, bf16[2,80,512]{2,1,0:T(8,128)(2,1)S(1)}, u32[]{:S(2)}, u32[]{:S(2)}) collective-permute-start(bf16[2,80,512]{2,1,0:T(8,128)(2,1)S(1)} %collective-permute-done.35.refs_5_), channel_id=1, source_target_pairs={{0,1},{1,0},{2,3},{3,2},{4,5},{5,4},{6,7},{7,6},{8,9},{9,8},{10,11... | collective-permute-start | bytes 491528 | tf_op jit(solution)/shard_map/ppermute | solution.py:343
  113.8 13.8 %collective-permute-start.44 = (bf16[1,80,512]{2,1,0:T(8,128)(2,1)S(1)}, bf16[1,80,512]{2,1,0:T(8,128)(2,1)S(1)}, u32[]{:S(2)}, u32[]{:S(2)}) collective-permute-start(bf16[1,80,512]{2,1,0:T(8,128)(2,1)S(1)} %shard_map.76.refs_2_), channel_id=1, source_target_pairs={{0,1},{1,0},{2,3},{3,2},{4,5},{5,4},{6,7},{7,6},{8,9},{9,8},{10,11... | collective-permute-start | bytes 245768 | tf_op jit(solution)/shard_map/ppermute | solution.py:342
  117.1 10.4 %collective-permute-start.45 = (bf16[1,80,512]{2,1,0:T(8,128)(2,1)S(1)}, bf16[1,80,512]{2,1,0:T(8,128)(2,1)S(1)}, u32[]{:S(2)}, u32[]{:S(2)}) collective-permute-start(bf16[1,80,512]{2,1,0:T(8,128)(2,1)S(1)} %collective-permute-done.43.refs_3_), channel_id=1, source_target_pairs={{0,1},{1,0},{2,3},{3,2},{4,5},{5,4},{6,7},{7,6},{8,9},{9,8},{10,11... | collective-permute-start | bytes 245768 | tf_op jit(solution)/shard_map/ppermute | solution.py:343
  (23 other events, 141.7 us)

commit v2 on v1

--- a/solution.py
+++ b/solution.py
@@ -56,13 +56,15 @@
     return weights
 
 
-def grad_kernel(where, *refs, blocks, phases, olds):
+def grad_kernel(where, *refs, blocks, phases, olds, pairs_of=None, offsets=None):
     news = len(blocks)
     xs = refs[: 2 * news]
     errors = refs[2 * news : 2 * news + 4 * phases]
     old = refs[2 * news + 4 * phases : 2 * news + 4 * phases + olds]
-    new = refs[2 * news + 4 * phases + olds : 3 * news + 4 * phases + olds]
-    sums = refs[-1]
+    rest = refs[2 * news + 4 * phases + olds :]
+    done = rest[: -news - 1]
+    new = rest[-news - 1 : -1]
+    sums = rest[-1]
     second = where[1] & 1 == 1
     upper = where[1] >> 1 == 1
     for n, ends in enumerate(blocks):
@@ -95,8 +97,12 @@
     totals = lax.fori_loop(
         0, features // 8, body, tuple(jnp.zeros((8, 128), jnp.float32) for _ in pairs), unroll=4
     )
-    for k in range(len(pairs)):
-        sums[k] = totals[k]
+    if offsets is None:
+        for k in range(len(pairs)):
+            sums[k] = totals[k]
+    else:
+        parts = [ref[k] for ref in done for k in range(ref.shape[0])] + list(totals)
+        sums[...] = placed(where, parts, pairs_of, offsets)
 
 
 def ring_replica(index, count):
@@ -112,22 +118,16 @@
     return ring_replica(jnp.where(index >= count, index - count, index), count)
 
 
-def place_kernel(where, *refs, pairs, offsets):
-    out = refs[-1]
-    count = len(offsets)
-    ids = [replica_at(where[0], offset, count) for offset in offsets]
+def placed(where, parts, pairs, offsets):
+    ids = [replica_at(where[0], offset, len(offsets)) for offset in offsets]
     row = lax.broadcasted_iota(jnp.int32, (8, 128), 0)
     column = lax.broadcasted_iota(jnp.int32, (8, 128), 1)
     tile = jnp.zeros((8, 128), jnp.float32)
-    at = 0
-    for ref in refs[:-1]:
-        for k in range(ref.shape[0]):
-            i, j = pairs[at]
-            at += 1
-            total = jnp.sum(ref[k], axis=(0, 1), keepdims=True)
-            here = ((row == ids[i]) & (column == ids[j])) | ((row == ids[j]) & (column == ids[i]))
-            tile = jnp.where(here, total, tile)
-    out[...] = tile
+    for part, (i, j) in zip(parts, pairs):
+        total = jnp.sum(part, axis=(0, 1), keepdims=True)
+        here = ((row == ids[i]) & (column == ids[j])) | ((row == ids[j]) & (column == ids[i]))
+        tile = jnp.where(here, total, tile)
+    return tile
 
 
 def combine_kernel(where, products, weight, *refs, offsets, parts):
@@ -320,7 +320,9 @@
             shape = ((len(xs), quarter, features), inputs.dtype)
             outgoing = local_call(pick_kernel, (shape,), where, *xs)
         others = [lax.ppermute(x, "shard", swap_core) for x in outgoing]
-        keep, send = local_call(outputs_kernel, (part, part), where, *xs, *others, weight_b, weight_other)
+        keep, send = local_call(
+            outputs_kernel, (part, part), where, *xs, *others, weight_b, weight_other
+        )
         summed += [(keep, lax.ppermute(send, "shard", swap_y))]
 
     errors = []
@@ -346,7 +348,7 @@
     grads = []
     sums = []
     pairs = []
-    for group in groups:
+    for m, group in enumerate(groups):
         olds = len(grads)
         needed = sorted({errors_at[offset, half][0] for offset in group for half in range(2)})
         blocks = tuple(
@@ -354,21 +356,29 @@
             for offset in group
         )
         fresh = [(i, olds + n) for n in range(len(group)) for i in range(olds + n + 1)]
+        pairs += fresh
+        last = m == len(groups) - 1
         made = local_call(
-            functools.partial(grad_kernel, blocks=blocks, phases=len(needed), olds=olds),
-            ((weight.shape, jnp.float32),) * len(group) + (((len(fresh), 8, 128), jnp.float32),),
+            functools.partial(
+                grad_kernel,
+                blocks=blocks,
+                phases=len(needed),
+                olds=olds,
+                pairs_of=tuple(pairs) if last else None,
+                offsets=offsets if last else None,
+            ),
+            ((weight.shape, jnp.float32),) * len(group)
+            + (((8, 128) if last else (len(fresh), 8, 128), jnp.float32),),
             where,
             *[halves[offset][half] for offset in group for half in range(2)],
             *[part for phase in needed for part in errors[phase]],
             *grads,
-        )
-        pairs += fresh
+            *(sums if last else ()),
+        )
         grads = grads + list(made[: len(group)])
         sums.append(made[len(group)])
 
-    (products,) = local_call(
-        functools.partial(place_kernel, pairs=pairs, offsets=offsets), (((8, 128), jnp.float32),), where, *sums
-    )
+    products = sums[-1]
     products = products + lax.ppermute(products, "shard", swap_core)
     products = products + lax.ppermute(products, "shard", swap_y)
     bit = 1

time: 151 us -> 150 us (level)
  waiting for transfers between devices: 79.9 us -> 72 us
  starting transfers between devices: 36.3 us -> 43.4 us
    ppermute x4, waiting for transfers between devices: 9.46 us -> 0.06 us  [ring_path(): d = lax.ppermute(from_right[-1][1], 'rep', left)]
    ppermute x3, waiting for transfers between devices: 1.04 us -> 9.45 us  [ring_path(): b = None if last else lax.ppermute(from_left[-1][1], 'rep', right)]
    ppermute x3, starting transfers between devices: 1.93 us -> 5.63 us  [ring_path(): b = None if last else lax.ppermute(from_left[-1][1], 'rep', right)]
    ppermute x3, waiting for transfers between devices: 14.9 us -> 11.4 us  [ring_path(): lax.ppermute(block, 'rep', [(r, r ^ 1 << i) for r in range(count)])]
    ppermute x3, starting transfers between devices: 2.85 us -> 5.52 us  [ring_path(): lax.ppermute(block, 'rep', [(r, r ^ 1 << i) for r in range(count)])]
    ppermute x3, waiting for transfers between devices: 9.19 us -> 6.67 us  [ring_path(): lax.ppermute(products, 'rep', [(i, i ^ bit) for i in range(count)])]
    ppermute x3, starting transfers between devices: 2.56 us -> 5.05 us  [ring_path(): lax.ppermute(products, 'rep', [(i, i ^ bit) for i in range(count)])]
    ppermute x4, starting transfers between devices: 3.6 us -> 1.63 us  [ring_path(): d = lax.ppermute(from_right[-1][1], 'rep', left)]
  transfers between devices with their start and end apart: 51 -> 51, of which waited for: 22 -> 23; matrix products, arithmetic and copies ran while one was open for 0% -> 0% of each run, Pallas kernels for 16% -> 16%
where the time goes in v2:
time: 150 us
  waiting for transfers between devices  72 us (48%)
  starting transfers between devices  43.4 us (29%)
  Pallas kernels  30.1 us (20%)
  local copies, waits for them, and re-layouts  3.37 us (2%)
    pallas_call x19, Pallas kernels, local_call(): pl.pallas_call(kernel, in_specs=[pl.BlockSpec(memory_space=pltpu.SMEM)] +...  25.7 us
    ppermute x6, waiting for transfers between devices, ring_path(): summed += [(keep, lax.ppermute(send, 'shard', swap_y))]  17.5 us
    ppermute x3, waiting for transfers between devices, ring_path(): lax.ppermute(block, 'rep', [(r, r ^ 1 << i) for r in range(count)])  11.4 us
    ppermute x3, waiting for transfers between devices, ring_path(): c = None if last else lax.ppermute(from_right[-1][0], 'rep', left)  11 us
    ppermute x3, waiting for transfers between devices, ring_path(): b = None if last else lax.ppermute(from_left[-1][1], 'rep', right)  9.45 us
    ppermute x4, waiting for transfers between devices, ring_path(): across = lax.ppermute(error, 'shard', swap_y)  9.04 us
    ppermute x6, starting transfers between devices, ring_path(): summed += [(keep, lax.ppermute(send, 'shard', swap_y))]  7.29 us
    ppermute x3, waiting for transfers between devices, ring_path(): lax.ppermute(products, 'rep', [(i, i ^ bit) for i in range(count)])  6.67 us
  transfers between devices with their start and end apart: 51, of which 23 were waited for; matrix products, arithmetic and copies ran while one was open for 0% of the time, Pallas kernels for 16%

profile of v2, /device:TPU:0, one launch (start us, length us, event | category | flops | bytes accessed | tf_op | source)
XLA Modules:
  0.0 150.1 jit_solution(11382846297900082327)
XLA Ops:
  2.3 2.6 %collective-permute-start.18 = (bf16[160,1024]{1,0:T(8,128)(2,1)S(1)}, bf16[160,1024]{1,0:T(8,128)(2,1)S(1)}, u32[]{:S(2)}, u32[]{:S(2)}) collective-permute-start(bf16[160,1024]{1,0:T(8,128)(2,1)S(1)} %get-tuple-element.50.refs_1_), channel_id=1, source_target_pairs={{0,8},{8,16},{16,24},{24,28},{28,20},{20,12},{12,4},{4,0},{1,9},{9... | collective-permute-start | bytes 983048 | tf_op jit(solution)/shard_map/ppermute | solution.py:273
  5.1 1.8 %collective-permute-start.12 = (s32[1,80]{1,0:T(1,128)}, s32[1,80]{1,0:T(1,128)S(1)}, u32[]{:S(2)}, u32[]{:S(2)}) collective-permute-start(s32[1,80]{1,0:T(1,128)} %bitcast.3), channel_id=1, source_target_pairs={{0,4},{4,0},{8,12},{12,8},{16,20},{20,16},{24,28},{28,24},{1,5},{5... | collective-permute-start | bytes 968 | tf_op jit(solution)/shard_map/ppermute | solution.py:295
  7.0 6.3 %collective-permute-done.12.refs_1_ = s32[1,80]{1,0:T(1,128)S(1)} collective-permute-done((s32[1,80]{1,0:T(1,128)}, s32[1,80]{1,0:T(1,128)S(1)}, u32[]{:S(2)}, u32[]{:S(2)}) %collective-permute-start.12) | collective-permute-done | bytes 352 | tf_op jit(solution)/shard_map/ppermute | solution.py:295
  14.5 3.6 %collective-permute-done.13.refs_2_ = s32[2,80]{1,0:T(2,128)S(1)} collective-permute-done((s32[2,80]{1,0:T(2,128)S(1)}, s32[2,80]{1,0:T(2,128)S(1)}, u32[]{:S(2)}, u32[]{:S(2)}) %collective-permute-start.13) | collective-permute-done | bytes 672 | tf_op jit(solution)/shard_map/ppermute | solution.py:295
  18.7 3.7 %collective-permute-start.14 = (s32[4,80]{1,0:T(4,128)S(1)}, s32[4,80]{1,0:T(4,128)S(1)}, u32[]{:S(2)}, u32[]{:S(2)}) collective-permute-start(s32[4,80]{1,0:T(4,128)S(1)} %shard_map.62), channel_id=1, source_target_pairs={{0,16},{4,20},{8,24},{12,28},{16,0},{20,4},{24,8},{28,12},{1,17},{... | collective-permute-start | bytes 3848 | tf_op jit(solution)/shard_map/ppermute | solution.py:295
  26.0 2.0 %collective-permute-start.28 = (bf16[160,1024]{1,0:T(8,128)(2,1)S(1)}, bf16[160,1024]{1,0:T(8,128)(2,1)S(1)}, u32[]{:S(2)}, u32[]{:S(2)}) collective-permute-start(bf16[160,1024]{1,0:T(8,128)(2,1)S(1)} %collective-permute-done.18.refs_3_), channel_id=1, source_target_pairs={{0,8},{8,16},{16,24},{24,28},{28,20},{20,12},{12,4},{4,0},{1,9},{9... | collective-permute-start | bytes 983048 | tf_op jit(solution)/shard_map/ppermute | solution.py:273
  28.1 1.6 %copy-done = f32[1024,512]{1,0:T(8,128)S(1)} copy-done((f32[1024,512]{1,0:T(8,128)S(1)}, f32[1024,512]{1,0:T(8,128)}, u32[]{:S(2)}) %copy-start) | copy-done | bytes 2097176
  30.4 4.2 %collective-permute-done.19.refs_2_.refs_4_ = bf16[160,1024]{1,0:T(8,128)(2,1)S(1)} collective-permute-done((bf16[160,1024]{1,0:T(8,128)(2,1)S(1)}, bf16[160,1024]{1,0:T(8,128)(2,1)S(1)}, u32[]{:S(2)}, u32[]{:S(2)}) %collective-permute-start.19) | collective-permute-done | bytes 327712 | tf_op jit(solution)/shard_map/ppermute | solution.py:274
  36.6 6.0 %collective-permute-done.28.refs_3_.refs_1_ = bf16[160,1024]{1,0:T(8,128)(2,1)S(1)} collective-permute-done((bf16[160,1024]{1,0:T(8,128)(2,1)S(1)}, bf16[160,1024]{1,0:T(8,128)(2,1)S(1)}, u32[]{:S(2)}, u32[]{:S(2)}) %collective-permute-start.28) | collective-permute-done | bytes 327712 | tf_op jit(solution)/shard_map/ppermute | solution.py:273
  45.9 3.2 %collective-permute-done.1.refs_0_ = bf16[160,1024]{1,0:T(8,128)(2,1)S(1)} collective-permute-done((bf16[160,1024]{1,0:T(8,128)(2,1)S(1)}, bf16[160,1024]{1,0:T(8,128)(2,1)S(1)}, u32[]{:S(2)}, u32[]{:S(2)}) %collective-permute-start.1) | collective-permute-done | bytes 327712 | tf_op jit(solution)/shard_map/ppermute | solution.py:271
  50.6 3.4 %collective-permute-done.35.refs_1_ = bf16[160,1024]{1,0:T(8,128)(2,1)S(1)} collective-permute-done((bf16[160,1024]{1,0:T(8,128)(2,1)S(1)}, bf16[160,1024]{1,0:T(8,128)(2,1)S(1)}, u32[]{:S(2)}, u32[]{:S(2)}) %collective-permute-start.35) | collective-permute-done | bytes 327712 | tf_op jit(solution)/shard_map/ppermute | solution.py:273
  55.7 6.1 %collective-permute-done.36.refs_0_.refs_2_ = bf16[160,1024]{1,0:T(8,128)(2,1)S(1)} collective-permute-done((bf16[160,1024]{1,0:T(8,128)(2,1)S(1)}, bf16[160,1024]{1,0:T(8,128)(2,1)S(1)}, u32[]{:S(2)}, u32[]{:S(2)}) %collective-permute-start.36) | collective-permute-done | bytes 327712 | tf_op jit(solution)/shard_map/ppermute | solution.py:274
  72.4 7.4 %collective-permute-done.22.refs_1_ = f32[1,80,512]{2,1,0:T(8,128)S(1)} collective-permute-done((f32[1,80,512]{2,1,0:T(8,128)S(1)}, f32[1,80,512]{2,1,0:T(8,128)S(1)}, u32[]{:S(2)}, u32[]{:S(2)}) %collective-permute-start.22) | collective-permute-done | bytes 163872 | tf_op jit(solution)/shard_map/ppermute | solution.py:326
  83.2 1.6 %collective-permute-start.31 = (f32[2,80,512]{2,1,0:T(8,128)S(1)}, f32[2,80,512]{2,1,0:T(8,128)S(1)}, u32[]{:S(2)}, u32[]{:S(2)}) collective-permute-start(f32[2,80,512]{2,1,0:T(8,128)S(1)} %get-tuple-element.36), channel_id=1, source_target_pairs={{0,2},{1,3},{2,0},{3,1},{4,6},{5,7},{6,4},{7,5},{8,10},{9,11},{10,... | collective-permute-start | bytes 983048 | tf_op jit(solution)/shard_map/ppermute | solution.py:326
  88.3 2.0 %collective-permute-done.39.refs_1_ = f32[1,80,512]{2,1,0:T(8,128)S(1)} collective-permute-done((f32[1,80,512]{2,1,0:T(8,128)S(1)}, f32[1,80,512]{2,1,0:T(8,128)S(1)}, u32[]{:S(2)}, u32[]{:S(2)}) %collective-permute-start.39) | collective-permute-done | bytes 163872 | tf_op jit(solution)/shard_map/ppermute | solution.py:326
  90.9 6.4 %collective-permute-done.31.refs_1_ = f32[2,80,512]{2,1,0:T(8,128)S(1)} collective-permute-done((f32[2,80,512]{2,1,0:T(8,128)S(1)}, f32[2,80,512]{2,1,0:T(8,128)S(1)}, u32[]{:S(2)}, u32[]{:S(2)}) %collective-permute-start.31) | collective-permute-done | bytes 327712 | tf_op jit(solution)/shard_map/ppermute | solution.py:326
  101.1 1.6 %collective-permute-start.11 = (f32[1,80,512]{2,1,0:T(8,128)S(1)}, f32[1,80,512]{2,1,0:T(8,128)S(1)}, u32[]{:S(2)}, u32[]{:S(2)}) collective-permute-start(f32[1,80,512]{2,1,0:T(8,128)S(1)} %get-tuple-element.27), channel_id=1, source_target_pairs={{0,2},{1,3},{2,0},{3,1},{4,6},{5,7},{6,4},{7,5},{8,10},{9,11},{10,... | collective-permute-start | bytes 491528 | tf_op jit(solution)/shard_map/ppermute | solution.py:326
  103.2 2.9 %collective-permute-done.32.refs_5_ = bf16[2,80,512]{2,1,0:T(8,128)(2,1)S(1)} collective-permute-done((bf16[2,80,512]{2,1,0:T(8,128)(2,1)S(1)}, bf16[2,80,512]{2,1,0:T(8,128)(2,1)S(1)}, u32[]{:S(2)}, u32[]{:S(2)}) %collective-permute-start.32) | collective-permute-done | bytes 163872 | tf_op jit(solution)/shard_map/ppermute | solution.py:343
  106.1 3.0 %collective-permute-done.43.refs_5_ = bf16[2,80,512]{2,1,0:T(8,128)(2,1)S(1)} collective-permute-done((bf16[2,80,512]{2,1,0:T(8,128)(2,1)S(1)}, bf16[2,80,512]{2,1,0:T(8,128)(2,1)S(1)}, u32[]{:S(2)}, u32[]{:S(2)}) %collective-permute-start.43) | collective-permute-done | bytes 163872 | tf_op jit(solution)/shard_map/ppermute | solution.py:343
  109.2 1.8 %collective-permute-done.11.refs_1_ = f32[1,80,512]{2,1,0:T(8,128)S(1)} collective-permute-done((f32[1,80,512]{2,1,0:T(8,128)S(1)}, f32[1,80,512]{2,1,0:T(8,128)S(1)}, u32[]{:S(2)}, u32[]{:S(2)}) %collective-permute-start.11) | collective-permute-done | bytes 163872 | tf_op jit(solution)/shard_map/ppermute | solution.py:326
  113.3 3.1 %collective-permute-done.15.refs_3_ = bf16[1,80,512]{2,1,0:T(8,128)(2,1)S(1)} collective-permute-done((bf16[1,80,512]{2,1,0:T(8,128)(2,1)S(1)}, bf16[1,80,512]{2,1,0:T(8,128)(2,1)S(1)}, u32[]{:S(2)}, u32[]{:S(2)}) %collective-permute-start.15) | collective-permute-done | bytes 81952 | tf_op jit(solution)/shard_map/ppermute | solution.py:343
  116.4 3.3 %shard_map.68 = (f32[1024,512]{1,0:T(8,128)S(1)}, f32[1024,512]{1,0:T(8,128)S(1)}, f32[1024,512]{1,0:T(8,128)S(1)}, f32[6,8,128]{2,1,0:T(8,128)S(1)}) custom-call(s32[2]{0:T(128)S(1)} %pad_add_fusion.where, bf16[160,1024]{1,0:T(8,128)(2,1)S(1)} %get-tuple-element.51.refs_0_, bf16[160,1024]{1,0:T(8,128)(2,1)S(1)} %get-tuple-element.50.refs_1_, ...), custom_call_target="tpu_custom_call" | custom-call | tf_op jit(solution)/shard_map/pallas_call | solution.py:178
  119.8 3.2 %shard_map.72 = (f32[1024,512]{1,0:T(8,128)S(1)}, f32[1024,512]{1,0:T(8,128)S(1)}, f32[9,8,128]{2,1,0:T(8,128)S(1)}) custom-call(s32[2]{0:T(128)S(1)} %pad_add_fusion.where, bf16[160,1024]{1,0:T(8,128)(2,1)S(1)} %collective-permute-done.1.refs_0_, bf16[160,1024]{1,0:T(8,128)(2,1)S(1)} %collective-permute-done.28.refs_3_.refs_1_, ...), custom_call_target="tpu_custom_call" | custom-call | tf_op jit(solution)/shard_map/pallas_call | solution.py:178
  123.0 3.8 %shard_map.76 = (f32[1024,512]{1,0:T(8,128)S(1)}, f32[1024,512]{1,0:T(8,128)S(1)}, f32[13,8,128]{2,1,0:T(8,128)S(1)}) custom-call(s32[2]{0:T(128)S(1)} %pad_add_fusion.where, bf16[160,1024]{1,0:T(8,128)(2,1)S(1)} %collective-permute-done.2.refs_0_, bf16[160,1024]{1,0:T(8,128)(2,1)S(1)} %collective-permute-done.35.refs_1_, ...), custom_call_target="tpu_custom_call" | custom-call | tf_op jit(solution)/shard_map/pallas_call | solution.py:178
  126.9 3.0 %shard_map.77 = (f32[1024,512]{1,0:T(8,128)S(1)}, f32[8,128]{1,0:T(8,128)S(1)}) custom-call(s32[2]{0:T(128)S(1)} %pad_add_fusion.where, bf16[160,1024]{1,0:T(8,128)(2,1)S(1)} %collective-permute-done.3.refs_0_, bf16[160,1024]{1,0:T(8,128)(2,1)S(1)} %collective-permute-done.7.refs_1_, bf16[1,80,512]{2,1,0:T(8,128)(2,1)S(1)} %shard_map.63.refs_2_, ...), custom_call_target="tpu_custom_call" | custom-call | tf_op jit(solution)/shard_map/pallas_call | solution.py:178
  132.8 2.1 %collective-permute-done.47 = f32[8,128]{1,0:T(8,128)S(1)} collective-permute-done((f32[8,128]{1,0:T(8,128)S(1)}, f32[8,128]{1,0:T(8,128)S(1)}, u32[]{:S(2)}, u32[]{:S(2)}) %collective-permute-start.47) | collective-permute-done | bytes 4128 | tf_op jit(solution)/shard_map/ppermute | solution.py:383
  135.6 2.8 %collective-permute-done.48 = f32[8,128]{1,0:T(8,128)S(1)} collective-permute-done((f32[8,128]{1,0:T(8,128)S(1)}, f32[8,128]{1,0:T(8,128)S(1)}, u32[]{:S(2)}, u32[]{:S(2)}) %collective-permute-start.48) | collective-permute-done | bytes 4128 | tf_op jit(solution)/shard_map/ppermute | solution.py:386
  138.5 1.7 %collective-permute-start.49 = (f32[8,128]{1,0:T(8,128)S(1)}, f32[8,128]{1,0:T(8,128)S(1)}, u32[]{:S(2)}, u32[]{:S(2)}) collective-permute-start(f32[8,128]{1,0:T(8,128)S(1)} %add.17), channel_id=1, source_target_pairs={{0,8},{4,12},{8,0},{12,4},{16,24},{20,28},{24,16},{28,20},{1,9},{5... | collective-permute-start | bytes 12296 | tf_op jit(solution)/shard_map/ppermute | solution.py:386
  140.2 1.9 %collective-permute-done.49 = f32[8,128]{1,0:T(8,128)S(1)} collective-permute-done((f32[8,128]{1,0:T(8,128)S(1)}, f32[8,128]{1,0:T(8,128)S(1)}, u32[]{:S(2)}, u32[]{:S(2)}) %collective-permute-start.49) | collective-permute-done | bytes 4128 | tf_op jit(solution)/shard_map/ppermute | solution.py:386
  142.1 2.5 %collective-permute-start.50 = (f32[8,128]{1,0:T(8,128)S(1)}, f32[8,128]{1,0:T(8,128)S(1)}, u32[]{:S(2)}, u32[]{:S(2)}) collective-permute-start(f32[8,128]{1,0:T(8,128)S(1)} %add.18), channel_id=1, source_target_pairs={{0,16},{4,20},{8,24},{12,28},{16,0},{20,4},{24,8},{28,12},{1,17},{... | collective-permute-start | bytes 12296 | tf_op jit(solution)/shard_map/ppermute | solution.py:386
  144.6 2.0 %collective-permute-done.50 = f32[8,128]{1,0:T(8,128)S(1)} collective-permute-done((f32[8,128]{1,0:T(8,128)S(1)}, f32[8,128]{1,0:T(8,128)S(1)}, u32[]{:S(2)}, u32[]{:S(2)}) %collective-permute-start.50) | collective-permute-done | bytes 4128 | tf_op jit(solution)/shard_map/ppermute | solution.py:386
  146.6 3.4 %combine.1 = (f32[1024,512]{1,0:T(8,128)}, f32[1024,512]{1,0:T(8,128)}) custom-call(s32[2]{0:T(128)S(1)} %pad_add_fusion.where, f32[8,128]{1,0:T(8,128)S(1)} %add.19.products, f32[1024,512]{1,0:T(8,128)S(1)} %copy-done.1, f32[1024,512]{1,0:T(8,128)S(1)} %get-tuple-element.32.refs_8_.refs_6_.refs_0_, ...), custom_call_target="tpu_custom_call" | custom-call | tf_op jit(solution)/shard_map/combine/pallas_call | solution.py:392
  (106 shorter events, 45.0 us)
Async XLA Ops:
  1.7 23.3 %collective-permute-start.21 = (bf16[160,1024]{1,0:T(8,128)(2,1)S(1)}, bf16[160,1024]{1,0:T(8,128)(2,1)S(1)}, u32[]{:S(2)}, u32[]{:S(2)}) collective-permute-start(bf16[160,1024]{1,0:T(8,128)(2,1)S(1)} %get-tuple-element.50.refs_1_), channel_id=1, source_target_pairs={{0,1},{1,0},{2,3},{3,2},{4,5},{5,4},{6,7},{7,6},{8,9},{9,8},{10,11... | collective-permute-start | bytes 983048 | tf_op jit(solution)/shard_map/ppermute | solution.py:322
  2.3 23.7 %collective-permute-start.18 = (bf16[160,1024]{1,0:T(8,128)(2,1)S(1)}, bf16[160,1024]{1,0:T(8,128)(2,1)S(1)}, u32[]{:S(2)}, u32[]{:S(2)}) collective-permute-start(bf16[160,1024]{1,0:T(8,128)(2,1)S(1)} %get-tuple-element.50.refs_1_), channel_id=1, source_target_pairs={{0,8},{8,16},{16,24},{24,28},{28,20},{20,12},{12,4},{4,0},{1,9},{9... | collective-permute-start | bytes 983048 | tf_op jit(solution)/shard_map/ppermute | solution.py:273
  4.9 23.1 %collective-permute-start.4 = (bf16[160,1024]{1,0:T(8,128)(2,1)S(1)}, bf16[160,1024]{1,0:T(8,128)(2,1)S(1)}, u32[]{:S(2)}, u32[]{:S(2)}) collective-permute-start(bf16[160,1024]{1,0:T(8,128)(2,1)S(1)} %get-tuple-element.50.refs_1_), channel_id=1, source_target_pairs={{8,0},{16,8},{24,16},{28,24},{20,28},{12,20},{4,12},{0,4},{9,1},{1... | collective-permute-start | bytes 983048 | tf_op jit(solution)/shard_map/ppermute | solution.py:272
  4.9 25.4 %collective-permute-start.20 = (bf16[160,1024]{1,0:T(8,128)(2,1)S(1)}, bf16[160,1024]{1,0:T(8,128)(2,1)S(1)}, u32[]{:S(2)}, u32[]{:S(2)}) collective-permute-start(bf16[160,1024]{1,0:T(8,128)(2,1)S(1)} %get-tuple-element.51.refs_0_), channel_id=1, source_target_pairs={{0,1},{1,0},{2,3},{3,2},{4,5},{5,4},{6,7},{7,6},{8,9},{9,8},{10,11... | collective-permute-start | bytes 983048 | tf_op jit(solution)/shard_map/ppermute | solution.py:322
  23.9 10.7 %collective-permute-start.19 = (bf16[160,1024]{1,0:T(8,128)(2,1)S(1)}, bf16[160,1024]{1,0:T(8,128)(2,1)S(1)}, u32[]{:S(2)}, u32[]{:S(2)}) collective-permute-start(bf16[160,1024]{1,0:T(8,128)(2,1)S(1)} %get-tuple-element.51.refs_0_), channel_id=1, source_target_pairs={{8,0},{16,8},{24,16},{28,24},{20,28},{12,20},{4,12},{0,4},{9,1},{1... | collective-permute-start | bytes 983048 | tf_op jit(solution)/shard_map/ppermute | solution.py:274
  25.0 10.6 %collective-permute-start = (bf16[160,1024]{1,0:T(8,128)(2,1)S(1)}, bf16[160,1024]{1,0:T(8,128)(2,1)S(1)}, u32[]{:S(2)}, u32[]{:S(2)}) collective-permute-start(bf16[160,1024]{1,0:T(8,128)(2,1)S(1)} %get-tuple-element.51.refs_0_), channel_id=1, source_target_pairs={{0,8},{8,16},{16,24},{24,28},{28,20},{20,12},{12,4},{4,0},{1,9},{9... | collective-permute-start | bytes 983048 | tf_op jit(solution)/shard_map/ppermute | solution.py:271
  26.0 16.6 %collective-permute-start.28 = (bf16[160,1024]{1,0:T(8,128)(2,1)S(1)}, bf16[160,1024]{1,0:T(8,128)(2,1)S(1)}, u32[]{:S(2)}, u32[]{:S(2)}) collective-permute-start(bf16[160,1024]{1,0:T(8,128)(2,1)S(1)} %collective-permute-done.18.refs_3_), channel_id=1, source_target_pairs={{0,8},{8,16},{16,24},{24,28},{28,20},{20,12},{12,4},{4,0},{1,9},{9... | collective-permute-start | bytes 983048 | tf_op jit(solution)/shard_map/ppermute | solution.py:273
  28.1 16.2 %collective-permute-start.5 = (bf16[160,1024]{1,0:T(8,128)(2,1)S(1)}, bf16[160,1024]{1,0:T(8,128)(2,1)S(1)}, u32[]{:S(2)}, u32[]{:S(2)}) collective-permute-start(bf16[160,1024]{1,0:T(8,128)(2,1)S(1)} %collective-permute-done.4.refs_1_.refs_5_), channel_id=1, source_target_pairs={{8,0},{16,8},{24,16},{28,24},{20,28},{12,20},{4,12},{0,4},{9,1},{1... | collective-permute-start | bytes 983048 | tf_op jit(solution)/shard_map/ppermute | solution.py:272
  30.3 32.0 %collective-permute-start.10 = (bf16[1024,512]{1,0:T(8,128)(2,1)S(1)}, bf16[1024,512]{1,0:T(8,128)(2,1)S(1)}, u32[]{:S(2)}, u32[]{:S(2)}) collective-permute-start(bf16[1024,512]{1,0:T(8,128)(2,1)S(1)} %shard_map.59.refs_4_.refs_5_), channel_id=1, source_target_pairs={{0,1},{1,0},{2,3},{3,2},{4,5},{5,4},{6,7},{7,6},{8,9},{9,8},{10,11... | collective-permute-start | bytes 3145736 | tf_op jit(solution)/shard_map/ppermute | solution.py:313
  34.6 10.5 %collective-permute-start.29 = (bf16[160,1024]{1,0:T(8,128)(2,1)S(1)}, bf16[160,1024]{1,0:T(8,128)(2,1)S(1)}, u32[]{:S(2)}, u32[]{:S(2)}) collective-permute-start(bf16[160,1024]{1,0:T(8,128)(2,1)S(1)} %collective-permute-done.19.refs_2_.refs_4_), channel_id=1, source_target_pairs={{8,0},{16,8},{24,16},{28,24},{20,28},{12,20},{4,12},{0,4},{9,1},{1... | collective-permute-start | bytes 983048 | tf_op jit(solution)/shard_map/ppermute | solution.py:274
  35.6 13.5 %collective-permute-start.1 = (bf16[160,1024]{1,0:T(8,128)(2,1)S(1)}, bf16[160,1024]{1,0:T(8,128)(2,1)S(1)}, u32[]{:S(2)}, u32[]{:S(2)}) collective-permute-start(bf16[160,1024]{1,0:T(8,128)(2,1)S(1)} %collective-permute-done.refs_0_.refs_2_), channel_id=1, source_target_pairs={{0,8},{8,16},{16,24},{24,28},{28,20},{20,12},{12,4},{4,0},{1,9},{9... | collective-permute-start | bytes 983048 | tf_op jit(solution)/shard_map/ppermute | solution.py:271
  42.6 11.3 %collective-permute-start.35 = (bf16[160,1024]{1,0:T(8,128)(2,1)S(1)}, bf16[160,1024]{1,0:T(8,128)(2,1)S(1)}, u32[]{:S(2)}, u32[]{:S(2)}) collective-permute-start(bf16[160,1024]{1,0:T(8,128)(2,1)S(1)} %collective-permute-done.28.refs_3_.refs_1_), channel_id=1, source_target_pairs={{0,8},{8,16},{16,24},{24,28},{28,20},{20,12},{12,4},{4,0},{1,9},{9... | collective-permute-start | bytes 983048 | tf_op jit(solution)/shard_map/ppermute | solution.py:273
  44.2 18.0 %collective-permute-start.23 = (bf16[4,80,1024]{2,1,0:T(8,128)(2,1)S(1)}, bf16[4,80,1024]{2,1,0:T(8,128)(2,1)S(1)}, u32[]{:S(2)}, u32[]{:S(2)}) collective-permute-start(bf16[4,80,1024]{2,1,0:T(8,128)(2,1)S(1)} %shard_map.65), channel_id=1, source_target_pairs={{0,1},{1,0},{2,3},{3,2},{4,5},{5,4},{6,7},{7,6},{8,9},{9,8},{10,11... | collective-permute-start | bytes 1966088 | tf_op jit(solution)/shard_map/ppermute | solution.py:322
  45.0 10.6 %collective-permute-start.6 = (bf16[160,1024]{1,0:T(8,128)(2,1)S(1)}, bf16[160,1024]{1,0:T(8,128)(2,1)S(1)}, u32[]{:S(2)}, u32[]{:S(2)}) collective-permute-start(bf16[160,1024]{1,0:T(8,128)(2,1)S(1)} %collective-permute-done.5.refs_1_.refs_3_), channel_id=1, source_target_pairs={{8,0},{16,8},{24,16},{28,24},{20,28},{12,20},{4,12},{0,4},{9,1},{1... | collective-permute-start | bytes 983048 | tf_op jit(solution)/shard_map/ppermute | solution.py:272
  49.1 12.6 %collective-permute-start.36 = (bf16[160,1024]{1,0:T(8,128)(2,1)S(1)}, bf16[160,1024]{1,0:T(8,128)(2,1)S(1)}, u32[]{:S(2)}, u32[]{:S(2)}) collective-permute-start(bf16[160,1024]{1,0:T(8,128)(2,1)S(1)} %collective-permute-done.29.refs_2_), channel_id=1, source_target_pairs={{8,0},{16,8},{24,16},{28,24},{20,28},{12,20},{4,12},{0,4},{9,1},{1... | collective-permute-start | bytes 983048 | tf_op jit(solution)/shard_map/ppermute | solution.py:274
  55.6 25.6 %collective-permute-start.30 = (bf16[4,80,1024]{2,1,0:T(8,128)(2,1)S(1)}, bf16[4,80,1024]{2,1,0:T(8,128)(2,1)S(1)}, u32[]{:S(2)}, u32[]{:S(2)}) collective-permute-start(bf16[4,80,1024]{2,1,0:T(8,128)(2,1)S(1)} %shard_map.69), channel_id=1, source_target_pairs={{0,1},{1,0},{2,3},{3,2},{4,5},{5,4},{6,7},{7,6},{8,9},{9,8},{10,11... | collective-permute-start | bytes 1966088 | tf_op jit(solution)/shard_map/ppermute | solution.py:322
  63.4 19.8 %collective-permute-start.7 = (bf16[160,1024]{1,0:T(8,128)(2,1)S(1)}, bf16[160,1024]{1,0:T(8,128)(2,1)S(1)}, u32[]{:S(2)}, u32[]{:S(2)}) collective-permute-start(bf16[160,1024]{1,0:T(8,128)(2,1)S(1)} %collective-permute-done.6.refs_1_.refs_3_), channel_id=1, source_target_pairs={{8,0},{16,8},{24,16},{28,24},{20,28},{12,20},{4,12},{0,4},{9,1},{1... | collective-permute-start | bytes 983048 | tf_op jit(solution)/shard_map/ppermute | solution.py:272
  65.5 19.2 %collective-permute-start.3 = (bf16[160,1024]{1,0:T(8,128)(2,1)S(1)}, bf16[160,1024]{1,0:T(8,128)(2,1)S(1)}, u32[]{:S(2)}, u32[]{:S(2)}) collective-permute-start(bf16[160,1024]{1,0:T(8,128)(2,1)S(1)} %collective-permute-done.2.refs_0_), channel_id=1, source_target_pairs={{0,8},{8,16},{16,24},{24,28},{28,20},{20,12},{12,4},{4,0},{1,9},{9... | collective-permute-start | bytes 983048 | tf_op jit(solution)/shard_map/ppermute | solution.py:271
  67.0 17.7 %collective-permute-start.24 = (f32[2,80,512]{2,1,0:T(8,128)S(1)}, f32[2,80,512]{2,1,0:T(8,128)S(1)}, u32[]{:S(2)}, u32[]{:S(2)}) collective-permute-start(f32[2,80,512]{2,1,0:T(8,128)S(1)} %get-tuple-element.31), channel_id=1, source_target_pairs={{0,2},{1,3},{2,0},{3,1},{4,6},{5,7},{6,4},{7,5},{8,10},{9,11},{10,... | collective-permute-start | bytes 983048 | tf_op jit(solution)/shard_map/ppermute | solution.py:326
  69.7 10.1 %collective-permute-start.22 = (f32[1,80,512]{2,1,0:T(8,128)S(1)}, f32[1,80,512]{2,1,0:T(8,128)S(1)}, u32[]{:S(2)}, u32[]{:S(2)}) collective-permute-start(f32[1,80,512]{2,1,0:T(8,128)S(1)} %get-tuple-element.29), channel_id=1, source_target_pairs={{0,2},{1,3},{2,0},{3,1},{4,6},{5,7},{6,4},{7,5},{8,10},{9,11},{10,... | collective-permute-start | bytes 491528 | tf_op jit(solution)/shard_map/ppermute | solution.py:326
  83.2 14.2 %collective-permute-start.31 = (f32[2,80,512]{2,1,0:T(8,128)S(1)}, f32[2,80,512]{2,1,0:T(8,128)S(1)}, u32[]{:S(2)}, u32[]{:S(2)}) collective-permute-start(f32[2,80,512]{2,1,0:T(8,128)S(1)} %get-tuple-element.36), channel_id=1, source_target_pairs={{0,2},{1,3},{2,0},{3,1},{4,6},{5,7},{6,4},{7,5},{8,10},{9,11},{10,... | collective-permute-start | bytes 983048 | tf_op jit(solution)/shard_map/ppermute | solution.py:326
  84.8 14.8 %collective-permute-start.9 = (bf16[160,1024]{1,0:T(8,128)(2,1)S(1)}, bf16[160,1024]{1,0:T(8,128)(2,1)S(1)}, u32[]{:S(2)}, u32[]{:S(2)}) collective-permute-start(bf16[160,1024]{1,0:T(8,128)(2,1)S(1)} %collective-permute-done.7.refs_1_), channel_id=1, source_target_pairs={{0,1},{1,0},{2,3},{3,2},{4,5},{5,4},{6,7},{7,6},{8,9},{9,8},{10,11... | collective-permute-start | bytes 983048 | tf_op jit(solution)/shard_map/ppermute | solution.py:322
  84.8 15.3 %collective-permute-start.8 = (bf16[160,1024]{1,0:T(8,128)(2,1)S(1)}, bf16[160,1024]{1,0:T(8,128)(2,1)S(1)}, u32[]{:S(2)}, u32[]{:S(2)}) collective-permute-start(bf16[160,1024]{1,0:T(8,128)(2,1)S(1)} %collective-permute-done.3.refs_0_), channel_id=1, source_target_pairs={{0,1},{1,0},{2,3},{3,2},{4,5},{5,4},{6,7},{7,6},{8,9},{9,8},{10,11... | collective-permute-start | bytes 983048 | tf_op jit(solution)/shard_map/ppermute | solution.py:322
  87.0 15.7 %collective-permute-start.25 = (bf16[3,80,512]{2,1,0:T(8,128)(2,1)S(1)}, bf16[3,80,512]{2,1,0:T(8,128)(2,1)S(1)}, u32[]{:S(2)}, u32[]{:S(2)}) collective-permute-start(bf16[3,80,512]{2,1,0:T(8,128)(2,1)S(1)} %shard_map.67.refs_6_), channel_id=1, source_target_pairs={{0,2},{1,3},{2,0},{3,1},{4,6},{5,7},{6,4},{7,5},{8,10},{9,11},{10,... | collective-permute-start | bytes 737288 | tf_op jit(solution)/shard_map/ppermute | solution.py:343
  90.3 12.4 %collective-permute-start.26 = (bf16[3,80,512]{2,1,0:T(8,128)(2,1)S(1)}, bf16[3,80,512]{2,1,0:T(8,128)(2,1)S(1)}, u32[]{:S(2)}, u32[]{:S(2)}) collective-permute-start(bf16[3,80,512]{2,1,0:T(8,128)(2,1)S(1)} %shard_map.67.refs_6_), channel_id=1, source_target_pairs={{0,1},{1,0},{2,3},{3,2},{4,5},{5,4},{6,7},{7,6},{8,9},{9,8},{10,11... | collective-permute-start | bytes 737288 | tf_op jit(solution)/shard_map/ppermute | solution.py:344
  101.1 9.8 %collective-permute-start.11 = (f32[1,80,512]{2,1,0:T(8,128)S(1)}, f32[1,80,512]{2,1,0:T(8,128)S(1)}, u32[]{:S(2)}, u32[]{:S(2)}) collective-permute-start(f32[1,80,512]{2,1,0:T(8,128)S(1)} %get-tuple-element.27), channel_id=1, source_target_pairs={{0,2},{1,3},{2,0},{3,1},{4,6},{5,7},{6,4},{7,5},{8,10},{9,11},{10,... | collective-permute-start | bytes 491528 | tf_op jit(solution)/shard_map/ppermute | solution.py:326
  102.7 10.4 %collective-permute-start.27 = (bf16[3,80,512]{2,1,0:T(8,128)(2,1)S(1)}, bf16[3,80,512]{2,1,0:T(8,128)(2,1)S(1)}, u32[]{:S(2)}, u32[]{:S(2)}) collective-permute-start(bf16[3,80,512]{2,1,0:T(8,128)(2,1)S(1)} %collective-permute-done.25.refs_7_), channel_id=1, source_target_pairs={{0,1},{1,0},{2,3},{3,2},{4,5},{5,4},{6,7},{7,6},{8,9},{9,8},{10,11... | collective-permute-start | bytes 737288 | tf_op jit(solution)/shard_map/ppermute | solution.py:345
  106.1 13.6 %collective-permute-start.34 = (bf16[2,80,512]{2,1,0:T(8,128)(2,1)S(1)}, bf16[2,80,512]{2,1,0:T(8,128)(2,1)S(1)}, u32[]{:S(2)}, u32[]{:S(2)}) collective-permute-start(bf16[2,80,512]{2,1,0:T(8,128)(2,1)S(1)} %collective-permute-done.32.refs_5_), channel_id=1, source_target_pairs={{0,1},{1,0},{2,3},{3,2},{4,5},{5,4},{6,7},{7,6},{8,9},{9,8},{10,11... | collective-permute-start | bytes 491528 | tf_op jit(solution)/shard_map/ppermute | solution.py:345
  109.1 13.9 %collective-permute-start.44 = (bf16[2,80,512]{2,1,0:T(8,128)(2,1)S(1)}, bf16[2,80,512]{2,1,0:T(8,128)(2,1)S(1)}, u32[]{:S(2)}, u32[]{:S(2)}) collective-permute-start(bf16[2,80,512]{2,1,0:T(8,128)(2,1)S(1)} %shard_map.75.refs_4_), channel_id=1, source_target_pairs={{0,1},{1,0},{2,3},{3,2},{4,5},{5,4},{6,7},{7,6},{8,9},{9,8},{10,11... | collective-permute-start | bytes 491528 | tf_op jit(solution)/shard_map/ppermute | solution.py:344
  110.9 12.1 %collective-permute-start.45 = (bf16[2,80,512]{2,1,0:T(8,128)(2,1)S(1)}, bf16[2,80,512]{2,1,0:T(8,128)(2,1)S(1)}, u32[]{:S(2)}, u32[]{:S(2)}) collective-permute-start(bf16[2,80,512]{2,1,0:T(8,128)(2,1)S(1)} %collective-permute-done.43.refs_5_), channel_id=1, source_target_pairs={{0,1},{1,0},{2,3},{3,2},{4,5},{5,4},{6,7},{7,6},{8,9},{9,8},{10,11... | collective-permute-start | bytes 491528 | tf_op jit(solution)/shard_map/ppermute | solution.py:345
  113.1 13.8 %collective-permute-start.16 = (bf16[1,80,512]{2,1,0:T(8,128)(2,1)S(1)}, bf16[1,80,512]{2,1,0:T(8,128)(2,1)S(1)}, u32[]{:S(2)}, u32[]{:S(2)}) collective-permute-start(bf16[1,80,512]{2,1,0:T(8,128)(2,1)S(1)} %shard_map.63.refs_2_), channel_id=1, source_target_pairs={{0,1},{1,0},{2,3},{3,2},{4,5},{5,4},{6,7},{7,6},{8,9},{9,8},{10,11... | collective-permute-start | bytes 245768 | tf_op jit(solution)/shard_map/ppermute | solution.py:344
  116.4 10.4 %collective-permute-start.17 = (bf16[1,80,512]{2,1,0:T(8,128)(2,1)S(1)}, bf16[1,80,512]{2,1,0:T(8,128)(2,1)S(1)}, u32[]{:S(2)}, u32[]{:S(2)}) collective-permute-start(bf16[1,80,512]{2,1,0:T(8,128)(2,1)S(1)} %collective-permute-done.15.refs_3_), channel_id=1, source_target_pairs={{0,1},{1,0},{2,3},{3,2},{4,5},{5,4},{6,7},{7,6},{8,9},{9,8},{10,11... | collective-permute-start | bytes 245768 | tf_op jit(solution)/shard_map/ppermute | solution.py:345
  (23 other events, 141.8 us)
